TPU v7x, 256 devices: a whole 4x4x8 slice. The times are simulated.
256 devices in a mesh: space: 32 (over z_hi, x, core), chan: 8 (over y, z_lo).
Axes of the slice: x: 4, y: 4, z: 8 (z_hi: 4, z_lo: 2; z = z_hi * 2 + z_lo), core: 2. Of those that a mesh axis runs over, the one named last changes fastest.
Arguments:
- patches: bfloat16 [64, 8192, 1024], P('chan', 'space'), may hold values from -6 to 6
- var_embed: float32 [64, 1024], P('chan'), may hold values from -3 to 3
- agg_query: float32 [1024], replicated, may hold values from -18 to 18
- pos_embed: bfloat16 [8192, 1024], P('space'), may hold values from -3 to 3
- gain_first: float32 [1024], replicated, may hold values from 0.1 to 1.9
- gain_second: float32 [1024], replicated, may hold values from 0.1 to 1.9
- w_qkv: bfloat16 [1024, 3, 1024], P(None, None, 'chan'), may hold values from -0.3 to 0.3
- w_out: bfloat16 [1024, 1024], P('chan'), may hold values from -0.1875 to 0.1875
- w_dec: bfloat16 [1024, 1024], replicated, may hold values from -0.1875 to 0.1875
- mod_scale: float32 [64, 1024], P('chan'), may hold values from -3 to 3
- mod_shift: float32 [64, 1024], P('chan'), may hold values from -3 to 3
Outputs:
- decoded: bfloat16 [64, 8192, 1024], P('chan', 'space')
All inputs are finite; a program needn't handle non-finite values.
Results may differ from a plain program's by a relative error of at most 0.025.
Values may be sent and summed in bfloat16 or wider, within the bound.
No kernel may reach another device: no remote copies, remote signals or barrier semaphores. Data moves between devices by JAX's collectives and lax.ppermute only.
A program may use at most 64 MiB of HBM per device.

v0:
```python
import functools
import math

import jax
import jax.numpy as jnp
from jax import lax
from jax.experimental import pallas as pl
from jax.experimental.pallas import tpu as pltpu
from jax.sharding import PartitionSpec as P


D = 1024
HEADS = 16
HEAD_DIM = D // HEADS
EPS = 1e-6
LOG2E = 1.4426950408889634
Z_HI, X, CORES = 4, 4, 2
F32, BF16 = jnp.float32, jnp.bfloat16

VMEM = pl.BlockSpec(memory_space=pltpu.VMEM)
ANY = pl.BlockSpec(memory_space=pl.ANY)
HBM = pl.BlockSpec(memory_space=pltpu.HBM)
PARAMS = pltpu.CompilerParams(vmem_limit_bytes=24 << 20)


def cost(flops, moved):
    return pl.CostEstimate(flops=flops, bytes_accessed=moved, transcendentals=0)


def shape(dims, dtype):
    return jax.ShapeDtypeStruct(dims, dtype)


def in_three(value):
    high = value.astype(BF16)
    rest = value - high.astype(F32)
    mid = rest.astype(BF16)
    low = (rest - mid.astype(F32)).astype(BF16)
    return high.astype(F32), mid.astype(F32), low.astype(F32)


def pool_kernel(patches, var_embed, query, out):
    count = patches.shape[0]
    rows = patches.shape[1]
    scaled = query[...] * (LOG2E / math.sqrt(D))
    shared = jnp.sum(var_embed[...] * scaled, -1, keepdims=True)
    logits = [
        jnp.sum(patches[v].astype(F32) * scaled, -1, keepdims=True) + shared[v : v + 1, :]
        for v in range(count)
    ]
    top = functools.reduce(jnp.maximum, logits)
    expo = [jnp.exp2(l - top) for l in logits]
    total = functools.reduce(jnp.add, expo)
    acc = jnp.zeros((rows, D), F32)
    for v in range(count):
        embedded = patches[v].astype(F32) + var_embed[v : v + 1, :]
        acc = acc + (expo[v] / total) * embedded
    out[0, :, :D] = acc.astype(BF16)
    high, mid, low = in_three(top + jnp.log2(total))
    lane = lax.broadcasted_iota(jnp.int32, (rows, 128), 1)
    packed = jnp.where(lane == 0, high, jnp.where(lane == 1, mid, jnp.where(lane == 2, low, 0.0)))
    out[0, :, D:] = packed.astype(BF16)


def pool(patches, var_embed, query, peers):
    count, rows, _ = patches.shape
    part = rows // peers
    return pl.pallas_call(
        pool_kernel,
        grid=(peers,),
        in_specs=[
            pl.BlockSpec((count, part, D), lambda i: (0, i, 0)),
            pl.BlockSpec((count, D), lambda i: (0, 0)),
            pl.BlockSpec((1, D), lambda i: (0, 0)),
        ],
        out_specs=pl.BlockSpec((1, part, D + 128), lambda i: (i, 0, 0)),
        out_shape=shape((peers, part, D + 128), BF16),
        cost_estimate=cost(16 << 20, 8 << 20),
        name="pool",
    )(patches, var_embed, query)


def merge_pool_kernel(parts, pos, resid):
    peers, rows, _ = parts.shape
    logs = [jnp.sum(parts[i, :, D:].astype(F32), -1, keepdims=True) for i in range(peers)]
    top = functools.reduce(jnp.maximum, logs)
    weights = [jnp.exp2(l - top) for l in logs]
    total = functools.reduce(jnp.add, weights)
    acc = jnp.zeros((rows, D), F32)
    for i in range(peers):
        acc = acc + (weights[i] / total) * parts[i, :, :D].astype(F32)
    start = pl.multiple_of(lax.axis_index("chan") * rows, rows)
    value = (acc + pos[pl.ds(start, rows), :].astype(F32)).astype(BF16)
    for i in range(peers):
        resid[i] = value


def merge_pool(parts, pos):
    peers, rows, _ = parts.shape
    return pl.pallas_call(
        merge_pool_kernel,
        in_specs=[VMEM, VMEM],
        out_specs=VMEM,
        out_shape=shape((peers, rows, D), BF16),
        compiler_params=PARAMS,
        cost_estimate=cost(4<< 20, 2<< 20),
        name="merge_pool",
    )(parts, pos)


def project_kernel(resid, gain, weight, w_out, mine, other, copies, sems):
    half = w_out.shape[0] // CORES
    start = pl.multiple_of(lax.axis_index("space") % CORES * half, half)
    share = w_out.at[pl.ds(start, half), :]
    moved = [pltpu.make_async_copy(share, copies.at[i], sems.at[i]) for i in range(copies.shape[0])]
    for copy in moved:
        copy.start()
    rows = resid.shape[0]
    value = resid[...].astype(F32)
    mean = jnp.mean(value * value, -1, keepdims=True)
    x = (value * lax.rsqrt(mean + EPS) * gain[...]).astype(BF16)
    q, k, v = (jnp.dot(x, weight[i], preferred_element_type=F32) for i in range(3))
    low = lax.broadcasted_iota(jnp.int32, (rows, 2 * HEAD_DIM), 1) < HEAD_DIM
    first = jnp.where(low, k, pltpu.roll(v, HEAD_DIM, 1))
    second = jnp.where(low, pltpu.roll(k, HEAD_DIM, 1), v)
    is_first = lax.axis_index("space") % CORES == 0
    turned = (q * (1.0 / math.sqrt(HEAD_DIM))).T
    top, bottom = turned[:HEAD_DIM], turned[HEAD_DIM:]
    half = rows // 2
    for ref, kv, qt in (
        (mine, jnp.where(is_first, first, second), jnp.where(is_first, top, bottom)),
        (other, jnp.where(is_first, second, first), jnp.where(is_first, bottom, top)),
    ):
        ref[:rows, :] = kv.astype(BF16)
        ref[rows : rows + HEAD_DIM, :] = qt[:, :half].astype(BF16)
        ref[rows + HEAD_DIM :, :] = qt[:, half:].astype(BF16)
    for copy in moved:
        copy.wait()


def project(resid, gain, weight, w_out, peers):
    rows = resid.shape[0]
    out = shape((rows + 2 * HEAD_DIM, 128), BF16)
    return pl.pallas_call(
        project_kernel,
        in_specs=[VMEM, VMEM, VMEM, VMEM],
        out_specs=(VMEM, VMEM, ANY),
        out_shape=(out, out, shape((peers, w_out.shape[0] // CORES, D), BF16)),
        scratch_shapes=[pltpu.SemaphoreType.DMA((peers,))],
        compiler_params=PARAMS,
        cost_estimate=cost(200 << 20, 4<< 20),
        name="project",
    )(resid, gain, weight, w_out)


def pair_kernel(mine, swapped, kv, qt):
    rows, turned = kv.shape[0] // 2, qt.shape[0] // 2
    kv[:rows, :] = mine[:rows, :]
    kv[rows:, :] = swapped[:rows, :]
    qt[:turned, :] = mine[rows:, :]
    qt[turned:, :] = swapped[rows:, :]


def pair(mine, swapped):
    rows = mine.shape[0] - 2 * HEAD_DIM
    return pl.pallas_call(
        pair_kernel,
        in_specs=[VMEM, VMEM],
        out_specs=(VMEM, VMEM),
        out_shape=(shape((2 * rows, 128), BF16), shape((4 * HEAD_DIM, 128), BF16)),
        compiler_params=PARAMS,
        cost_estimate=cost(1<< 20, 1<< 20),
        name="pair",
    )(mine, swapped)


def attend_kernel(k0, k1, k2, k3, q0, q1, q2, q3, o0, o1, o2, o3, keys, values_t):
    each = k0.shape[0]
    for i, ref in enumerate((k0, k1, k2, k3)):
        block = ref[...]
        keys[i * each : (i + 1) * each, :] = block
        values_t[:, i * each : (i + 1) * each] = block.T[HEAD_DIM:, :]
    scale = LOG2E
    zeros = jnp.zeros((HEAD_DIM, 256), BF16)
    for q, o in zip((q0, q1, q2, q3), (o0, o1, o2, o3)):
        for half in range(2):
            at = half * 2 * HEAD_DIM
            qt = jnp.concatenate([q[at : at + HEAD_DIM, :], q[at + HEAD_DIM : at + 2 * HEAD_DIM, :]], 1)
            qt = jnp.concatenate([qt, zeros], 0)
            scores = jnp.dot(keys[...], qt, preferred_element_type=F32)
            top = jnp.max(scores, 0, keepdims=True)
            probs = jnp.exp2((scores - top) * scale)
            total = jnp.sum(probs, 0, keepdims=True)
            acc = jnp.dot(values_t[...], probs.astype(BF16), preferred_element_type=F32)
            lanes = slice(half * 256, half * 256 + 256)
            o[:HEAD_DIM, lanes] = (acc / total).astype(BF16)
            high, mid, low = in_three(top * scale + jnp.log2(total))
            row = lax.broadcasted_iota(jnp.int32, (16, 256), 0)
            packed = jnp.where(row == 0, high, jnp.where(row == 1, mid, jnp.where(row == 2, low, 0.0)))
            o[HEAD_DIM:, lanes] = packed.astype(BF16)


def attend(key_pieces, query_pieces):
    each = key_pieces[0].shape[0]
    out = shape((HEAD_DIM + 16, each), BF16)
    return pl.pallas_call(
        attend_kernel,
        in_specs=[VMEM] * 8,
        out_specs=(VMEM,) * 4,
        out_shape=(out,) * 4,
        scratch_shapes=[
            pltpu.VMEM((4 * each, 128), BF16),
            pltpu.VMEM((HEAD_DIM, 4 * each), BF16),
        ],
        compiler_params=PARAMS,
        cost_estimate=cost(4 << 30, 8<< 20),
        name="attend",
    )(*key_pieces, *query_pieces)


def merge_heads_kernel(p0, p1, p2, p3, _, mine, other):
    refs = (p0, p1, p2, p3)
    logs = [jnp.sum(r[HEAD_DIM:, :].astype(F32), 0, keepdims=True) for r in refs]
    top = functools.reduce(jnp.maximum, logs)
    weights = [jnp.exp2(l - top) for l in logs]
    total = functools.reduce(jnp.add, weights)
    acc = jnp.zeros((HEAD_DIM, p0.shape[1]), F32)
    for r, w in zip(refs, weights):
        acc = acc + (w / total) * r[:HEAD_DIM, :].astype(F32)
    half = p0.shape[1] // 2
    mine[...] = acc[:, :half].astype(BF16)
    other[...] = acc[:, half:].astype(BF16)


def merge_heads(parts, after):
    width = parts[0].shape[1] // 2
    out = shape((HEAD_DIM, width), BF16)
    return pl.pallas_call(
        merge_heads_kernel,
        in_specs=[VMEM] * 4 + [ANY],
        out_specs=(VMEM, VMEM),
        out_shape=(out, out),
        compiler_params=PARAMS,
        cost_estimate=cost(1<< 20, 1<< 20),
        name="merge_heads",
    )(*parts, after)


def spread_kernel(mine, other, out):
    both = jnp.concatenate([mine[...].astype(F32), other[...].astype(F32)], 0)
    value = both.T.astype(BF16)
    for i in range(out.shape[0]):
        out[i] = value


def spread(mine, other, peers):
    return pl.pallas_call(
        spread_kernel,
        in_specs=[VMEM, VMEM],
        out_specs=VMEM,
        out_shape=shape((peers, mine.shape[1], 2 * HEAD_DIM), BF16),
        compiler_params=PARAMS,
        cost_estimate=cost(1<< 20, 1<< 20),
        name="spread",
    )(mine, other)


def decode_kernel(mixed, w_mine, w_other, resid, gain, scale, shift, w_dec, out, normed, weight, sem):
    step = pl.program_id(0)
    each = out.shape[0]

    @pl.when(step == 0)
    def _():
        copy = pltpu.make_async_copy(w_dec, weight, sem)
        copy.start()
        heads = jnp.concatenate([mixed[i] for i in range(mixed.shape[0])], 1)
        weights = [ref[i] for i in range(mixed.shape[0]) for ref in (w_mine, w_other)]
        value = jnp.dot(heads, jnp.concatenate(weights, 0), preferred_element_type=F32)
        value = value + resid[...].astype(F32)
        mean = jnp.mean(value * value, -1, keepdims=True)
        normed[...] = (value * lax.rsqrt(mean + EPS) * gain[...]).astype(BF16)
        copy.wait()

    parts = []
    for i in range(each):
        v = step * each + i
        row = (1.0 + scale[pl.ds(v, 1), :], shift[pl.ds(v, 1), :])
        parts.append((normed[...].astype(F32) * row[0] + row[1]).astype(BF16))
    modulated = jnp.concatenate(parts, 0)
    result = jnp.dot(modulated, weight[...], preferred_element_type=F32).astype(BF16)
    out[...] = result.reshape(out.shape)


def decode(mixed, w_mine, w_other, resid, gain, scale, shift, weight):
    count, rows = scale.shape[0], resid.shape[0]
    each = 2
    return pl.pallas_call(
        decode_kernel,
        grid=(count // each,),
        in_specs=[VMEM] * 7 + [HBM],
        out_specs=pl.BlockSpec((each, rows, D), lambda v: (v, 0, 0)),
        out_shape=shape((count, rows, D), BF16),
        scratch_shapes=[
            pltpu.VMEM((rows, D), BF16),
            pltpu.VMEM((D, D), BF16),
            pltpu.SemaphoreType.DMA(()),
        ],
        compiler_params=PARAMS,
        cost_estimate=cost(5<< 30, 8<< 20),
        name="decode",
    )(mixed, w_mine, w_other, resid, gain, scale, shift, weight)


def space_index(z, x, core):
    return (z * X + x) * CORES + core


def moves(step):
    return [
        (space_index(z, x, c), space_index(*step(z, x, c)))
        for z in range(Z_HI)
        for x in range(X)
        for c in range(CORES)
    ]


SWAP = moves(lambda z, x, c: (z, x, 1 - c))


def along_x(k):
    return moves(lambda z, x, c: (z, (x + k) % X, c))


def along_z(k):
    return moves(lambda z, x, c: ((z + k) % Z_HI, x, c))


def exchange(array):
    return lax.all_to_all(array, "chan", 0, 0, tiled=True)


def body(
    patches,
    var_embed,
    agg_query,
    pos_embed,
    gain_first,
    gain_second,
    w_qkv,
    w_out,
    w_dec,
    mod_scale,
    mod_shift,
):
    rows = patches.shape[1]
    peers = lax.axis_size("chan")

    parts = exchange(pool(patches, var_embed, agg_query.reshape(1, D), peers))
    resid = exchange(merge_pool(parts, pos_embed)).reshape(rows, D)

    mine, other, copies = project(
        resid, gain_first.reshape(1, D), w_qkv.transpose(1, 0, 2), w_out, peers
    )
    kv, qt = pair(mine, lax.ppermute(other, "space", SWAP))
    query_pieces = [qt] + [lax.ppermute(qt, "space", along_z(k)) for k in (2, 1, 3)]
    key_pieces = [kv] + [lax.ppermute(kv, "space", along_x(k)) for k in (2, 1, 3)]
    w_mine = exchange(copies)
    partial = attend(key_pieces, query_pieces)
    back = [partial[0]] + [
        lax.ppermute(p, "space", along_z(-k)) for p, k in zip(partial[1:], (2, 1, 3))
    ]
    mine, other = merge_heads(back, w_mine)
    w_other = lax.ppermute(w_mine, "space", SWAP)
    mixed = exchange(spread(mine, lax.ppermute(other, "space", SWAP), peers))
    gain = gain_second.reshape(1, D)
    return decode(mixed, w_mine, w_other, resid, gain, mod_scale, mod_shift, w_dec)


def solution(mesh):
    placed = (
        P("chan", "space", None),
        P("chan", None),
        P(),
        P("space", None),
        P(),
        P(),
        P(None, None, "chan"),
        P("chan", None),
        P(),
        P("chan", None),
        P("chan", None),
    )

    return jax.shard_map(
        body, mesh=mesh, in_specs=placed, out_specs=P("chan", "space", None), check_vma=False
    )
```

profile of v0, /device:TPU:2, one launch (start us, length us, event | category | flops | bytes accessed | tf_op | source)
XLA Modules:
  0.0 113.6 jit_solution(14385072302783542682)
XLA Ops:
  0.0 0.0 copy-start.1
  0.0 0.0 copy-start
  0.0 0.0 copy-start.2
  0.0 0.0 copy-start.3
  0.0 7.1 %pool.1 = bf16[8,32,1152]{2,1,0:T(8,128)(2,1)} custom-call(bf16[8,256,1024]{2,1,0:T(8,128)(2,1)} %patches.1, f32[8,1024]{1,0:T(8,128)} %var_embed.1, f32[1,1024]{1,0:T(1,128)} %bitcast.10), custom_call_target="tpu_custom_call" | custom-call | flops 16777216 | bytes 8388608 | tf_op jit(solution)/shard_map/pool/pallas_call | solution.py:68
  7.1 16.7 %all_to_all.20.parts = bf16[8,32,1152]{2,1,0:T(8,128)(2,1)S(1)} all-to-all(bf16[8,32,1152]{2,1,0:T(8,128)(2,1)} %pool.1), channel_id=1, replica_groups=mesh['space'=32,'chan'=8] {'chan'}, dimensions={0} | all-to-all | bytes 1179648 | tf_op jit(solution)/shard_map/all_to_all | solution.py:339
  23.9 0.0 copy-done.1
  23.9 0.3 merge_pool.1
  24.1 11.6 %all_to_all.21 = bf16[8,32,1024]{2,1,0:T(8,128)(2,1)S(1)} all-to-all(bf16[8,32,1024]{2,1,0:T(8,128)(2,1)S(1)} %merge_pool.1), channel_id=1, replica_groups=mesh['space'=32,'chan'=8] {'chan'}, dimensions={0} | all-to-all | bytes 1048576 | tf_op jit(solution)/shard_map/all_to_all | solution.py:339
  35.8 0.0 copy-done
  35.8 0.0 copy-done.2
  35.8 0.0 copy-done.3
  35.8 1.2 %project.1 = (bf16[384,128]{1,0:T(8,128)(2,1)S(1)}, bf16[384,128]{1,0:T(8,128)(2,1)S(1)}, bf16[8,64,1024]{2,1,0:T(8,128)(2,1)}) custom-call(bf16[256,1024]{1,0:T(8,128)(2,1)S(1)} %bitcast.5, f32[1,1024]{1,0:T(1,128)S(1)} %bitcast.8, bf16[3,1024,128]{2,1,0:T(8,128)(2,1)S(1)} %bitcast.7, bf16[128,1024]{1,0:T(8,128)(2,1)S(1)} %copy-done.2), custom_call_target="tpu_custom_call" | custom-call | flops 209715200 | bytes 4194304 | tf_op jit(solution)/shard_map/project/pallas_call | solution.py:144
  37.0 3.6 %all-to-all-start.2 = ((bf16[8,64,1024]{2,1,0:T(8,128)(2,1)}), bf16[8,64,1024]{2,1,0:T(8,128)(2,1)S(1)}, u32[]{:S(2)}, u32[]{:S(2)}) async-start(bf16[8,64,1024]{2,1,0:T(8,128)(2,1)} %get-tuple-element.24), calls=%async_computation.2 | async-start | bytes 2097152 | tf_op jit(solution)/shard_map/all_to_all | solution.py:339
  40.6 0.1 collective-permute-start
  40.7 1.3 %collective-permute-done.swapped = bf16[384,128]{1,0:T(8,128)(2,1)S(1)} collective-permute-done((bf16[384,128]{1,0:T(8,128)(2,1)S(1)}, bf16[384,128]{1,0:T(8,128)(2,1)S(1)}, u32[]{:S(2)}, u32[]{:S(2)}) %collective-permute-start) | collective-permute-done | bytes 98336 | tf_op jit(solution)/shard_map/ppermute | solution.py:364
  42.0 5.5 %collective-permute-start.6 = (bf16[256,128]{1,0:T(8,128)(2,1)S(1)}, bf16[256,128]{1,0:T(8,128)(2,1)S(1)}, u32[]{:S(2)}, u32[]{:S(2)}) collective-permute-start(bf16[256,128]{1,0:T(8,128)(2,1)S(1)} %get-tuple-element.19.q0), channel_id=1, source_target_pairs={{0,192},{8,200},{16,208},{24,216},{32,224},{40,232},{48,240},{56,2... | collective-permute-start | bytes 196616 | tf_op jit(solution)/shard_map/ppermute | solution.py:365
  47.5 0.0 copy-start.5
  47.5 0.0 copy-start.6
  47.5 0.0 copy-start.7
  47.5 0.5 collective-permute-start.3
  48.0 1.5 %collective-permute-start.2 = (bf16[512,128]{1,0:T(8,128)(2,1)S(1)}, bf16[512,128]{1,0:T(8,128)(2,1)S(1)}, u32[]{:S(2)}, u32[]{:S(2)}) collective-permute-start(bf16[512,128]{1,0:T(8,128)(2,1)S(1)} %get-tuple-element.18.k0), channel_id=1, source_target_pairs={{0,16},{8,24},{16,32},{24,40},{32,48},{40,56},{48,0},{56,8},{64,80... | collective-permute-start | bytes 393224 | tf_op jit(solution)/shard_map/ppermute | solution.py:366
  49.5 3.3 %collective-permute-start.1 = (bf16[512,128]{1,0:T(8,128)(2,1)S(1)}, bf16[512,128]{1,0:T(8,128)(2,1)S(1)}, u32[]{:S(2)}, u32[]{:S(2)}) collective-permute-start(bf16[512,128]{1,0:T(8,128)(2,1)S(1)} %get-tuple-element.18.k0), channel_id=1, source_target_pairs={{0,32},{8,40},{16,48},{24,56},{32,0},{40,8},{48,16},{56,24},{64,96... | collective-permute-start | bytes 393224 | tf_op jit(solution)/shard_map/ppermute | solution.py:366
  52.9 0.0 collective-permute-start.5
  52.9 0.0 collective-permute-done.6.q3
  52.9 3.8 %collective-permute-start.4 = (bf16[256,128]{1,0:T(8,128)(2,1)S(1)}, bf16[256,128]{1,0:T(8,128)(2,1)S(1)}, u32[]{:S(2)}, u32[]{:S(2)}) collective-permute-start(bf16[256,128]{1,0:T(8,128)(2,1)S(1)} %get-tuple-element.19.q0), channel_id=1, source_target_pairs={{0,128},{8,136},{16,144},{24,152},{32,160},{40,168},{48,176},{56,1... | collective-permute-start | bytes 196616 | tf_op jit(solution)/shard_map/ppermute | solution.py:365
  56.7 4.1 %collective-permute-done.5.q2 = bf16[256,128]{1,0:T(8,128)(2,1)S(1)} collective-permute-done((bf16[256,128]{1,0:T(8,128)(2,1)S(1)}, bf16[256,128]{1,0:T(8,128)(2,1)S(1)}, u32[]{:S(2)}, u32[]{:S(2)}) %collective-permute-start.5) | collective-permute-done | bytes 65568 | tf_op jit(solution)/shard_map/ppermute | solution.py:365
  60.8 0.0 all-to-all-done.2._.w_mine
  60.8 0.0 copy-start.4
  60.8 0.0 collective-permute-start.11
  60.8 0.9 collective-permute-done.4.q1
  61.7 0.0 collective-permute-done.3.k3
  61.7 0.0 collective-permute-done.2.k2
  61.7 0.0 collective-permute-done.1.k1
  61.7 10.3 %attend.1 = (bf16[80,512]{1,0:T(8,128)(2,1)S(1)}, bf16[80,512]{1,0:T(8,128)(2,1)S(1)}, bf16[80,512]{1,0:T(8,128)(2,1)S(1)}, bf16[80,512]{1,0:T(8,128)(2,1)S(1)}) custom-call(bf16[512,128]{1,0:T(8,128)(2,1)S(1)} %get-tuple-element.18.k0, bf16[512,128]{1,0:T(8,128)(2,1)S(1)} %collective-permute-done.1.k1, bf16[512,128]{1,0:T(8,128)(2,1)S(1)} %collective-permute-done.2.k2, ...), custom_call_target="tpu_custom_call" | custom-call | flops 4294967296 | bytes 8388608 | tf_op jit(solution)/shard_map/attend/pallas_call | solution.py:206
  72.1 3.6 %collective-permute-start.7 = (bf16[80,512]{1,0:T(8,128)(2,1)S(1)}, bf16[80,512]{1,0:T(8,128)(2,1)S(1)}, u32[]{:S(2)}, u32[]{:S(2)}) collective-permute-start(bf16[80,512]{1,0:T(8,128)(2,1)S(1)} %get-tuple-element.21), channel_id=1, source_target_pairs={{0,128},{8,136},{16,144},{24,152},{32,160},{40,168},{48,176},{56,1... | collective-permute-start | bytes 245768 | tf_op jit(solution)/shard_map/ppermute | solution.py:370
  75.7 2.9 %collective-permute-start.8 = (bf16[80,512]{1,0:T(8,128)(2,1)S(1)}, bf16[80,512]{1,0:T(8,128)(2,1)S(1)}, u32[]{:S(2)}, u32[]{:S(2)}) collective-permute-start(bf16[80,512]{1,0:T(8,128)(2,1)S(1)} %get-tuple-element.22), channel_id=1, source_target_pairs={{0,192},{8,200},{16,208},{24,216},{32,224},{40,232},{48,240},{56,2... | collective-permute-start | bytes 245768 | tf_op jit(solution)/shard_map/ppermute | solution.py:370
  78.6 0.0 collective-permute-start.9
  78.6 2.8 %collective-permute-done.7.p1 = bf16[80,512]{1,0:T(8,128)(2,1)S(1)} collective-permute-done((bf16[80,512]{1,0:T(8,128)(2,1)S(1)}, bf16[80,512]{1,0:T(8,128)(2,1)S(1)}, u32[]{:S(2)}, u32[]{:S(2)}) %collective-permute-start.7) | collective-permute-done | bytes 81952 | tf_op jit(solution)/shard_map/ppermute | solution.py:370
  81.4 2.2 %collective-permute-done.8.p2 = bf16[80,512]{1,0:T(8,128)(2,1)S(1)} collective-permute-done((bf16[80,512]{1,0:T(8,128)(2,1)S(1)}, bf16[80,512]{1,0:T(8,128)(2,1)S(1)}, u32[]{:S(2)}, u32[]{:S(2)}) %collective-permute-start.8) | collective-permute-done | bytes 81952 | tf_op jit(solution)/shard_map/ppermute | solution.py:370
  83.6 1.5 %collective-permute-done.9.p3 = bf16[80,512]{1,0:T(8,128)(2,1)S(1)} collective-permute-done((bf16[80,512]{1,0:T(8,128)(2,1)S(1)}, bf16[80,512]{1,0:T(8,128)(2,1)S(1)}, u32[]{:S(2)}, u32[]{:S(2)}) %collective-permute-start.9) | collective-permute-done | bytes 81952 | tf_op jit(solution)/shard_map/ppermute | solution.py:370
  85.1 0.1 merge_heads.1
  85.2 0.1 collective-permute-start.10
  85.3 1.2 %collective-permute-done.10.other = bf16[64,256]{1,0:T(8,128)(2,1)S(1)} collective-permute-done((bf16[64,256]{1,0:T(8,128)(2,1)S(1)}, bf16[64,256]{1,0:T(8,128)(2,1)S(1)}, u32[]{:S(2)}, u32[]{:S(2)}) %collective-permute-start.10) | collective-permute-done | bytes 32800 | tf_op jit(solution)/shard_map/ppermute | solution.py:374
  86.5 0.1 spread.1
  86.7 19.7 %all_to_all.22.mixed = bf16[8,256,128]{2,1,0:T(8,128)(2,1)S(1)} all-to-all(bf16[8,256,128]{2,1,0:T(8,128)(2,1)S(1)} %spread.1), channel_id=1, replica_groups=mesh['space'=32,'chan'=8] {'chan'}, dimensions={0} | all-to-all | bytes 1048576 | tf_op jit(solution)/shard_map/all_to_all | solution.py:339
  106.3 0.0 collective-permute-done.11.w_other
  106.3 0.0 copy-done.5
  106.3 0.0 copy-done.6
  106.3 0.0 copy-done.7
  106.3 0.0 copy-done.4
  106.4 7.1 %decode.1 = bf16[8,256,1024]{2,1,0:T(8,128)(2,1)} custom-call(bf16[8,256,128]{2,1,0:T(8,128)(2,1)S(1)} %all_to_all.22.mixed, bf16[8,64,1024]{2,1,0:T(8,128)(2,1)S(1)} %all-to-all-done.2._.w_mine, bf16[8,64,1024]{2,1,0:T(8,128)(2,1)S(1)} %collective-permute-done.11.w_other, bf16[256,1024]{1,0:T(8,128)(2,1)S(1)} %bitcast.6, f32[1,1024]{1,0:T(1,128)S(1)} %bitcast.9, ...), custom_call_target="tpu_custom_call" | custom-call | flops 5368709120 | bytes 8388608 | tf_op jit(solution)/shard_map/decode/pallas_call | solution.py:297
  (1 shorter events, 0.0 us)
Async XLA Ops:
  0.0 23.9 %copy-start.1 = (bf16[256,1024]{1,0:T(8,128)(2,1)S(1)}, bf16[256,1024]{1,0:T(8,128)(2,1)}, u32[]{:S(2)}) copy-start(bf16[256,1024]{1,0:T(8,128)(2,1)} %pos.1) | copy-start | bytes 1572868
  0.0 35.8 %copy-start = (bf16[1024,3,128]{2,0,1:T(8,128)(2,1)S(1)}, bf16[1024,3,128]{2,0,1:T(8,128)(2,1)}, u32[]{:S(2)}) copy-start(bf16[1024,3,128]{2,0,1:T(8,128)(2,1)} %param.17) | copy-start | bytes 2359300
  0.0 35.8 %copy-start.2 = (bf16[128,1024]{1,0:T(8,128)(2,1)S(1)}, bf16[128,1024]{1,0:T(8,128)(2,1)}, u32[]{:S(2)}) copy-start(bf16[128,1024]{1,0:T(8,128)(2,1)} %w_out.1) | copy-start | bytes 786436
  0.0 35.8 %copy-start.3 = (f32[1024]{0:T(1024)S(1)}, f32[1024]{0:T(1024)}, u32[]{:S(2)}) copy-start(f32[1024]{0:T(1024)} %param.15) | copy-start | bytes 12292
  37.0 23.7 %all-to-all-start.2 = ((bf16[8,64,1024]{2,1,0:T(8,128)(2,1)}), bf16[8,64,1024]{2,1,0:T(8,128)(2,1)S(1)}, u32[]{:S(2)}, u32[]{:S(2)}) async-start(bf16[8,64,1024]{2,1,0:T(8,128)(2,1)} %get-tuple-element.24), calls=%async_computation.2 | async-start | bytes 2097152 | tf_op jit(solution)/shard_map/all_to_all | solution.py:339
  40.6 1.4 %collective-permute-start = (bf16[384,128]{1,0:T(8,128)(2,1)S(1)}, bf16[384,128]{1,0:T(8,128)(2,1)S(1)}, u32[]{:S(2)}, u32[]{:S(2)}) collective-permute-start(bf16[384,128]{1,0:T(8,128)(2,1)S(1)} %get-tuple-element.17), channel_id=1, source_target_pairs={{0,8},{8,0},{16,24},{24,16},{32,40},{40,32},{48,56},{56,48},{64,72... | collective-permute-start | bytes 294920 | tf_op jit(solution)/shard_map/ppermute | solution.py:364
  42.0 10.9 %collective-permute-start.6 = (bf16[256,128]{1,0:T(8,128)(2,1)S(1)}, bf16[256,128]{1,0:T(8,128)(2,1)S(1)}, u32[]{:S(2)}, u32[]{:S(2)}) collective-permute-start(bf16[256,128]{1,0:T(8,128)(2,1)S(1)} %get-tuple-element.19.q0), channel_id=1, source_target_pairs={{0,192},{8,200},{16,208},{24,216},{32,224},{40,232},{48,240},{56,2... | collective-permute-start | bytes 196616 | tf_op jit(solution)/shard_map/ppermute | solution.py:365
  47.5 58.8 %copy-start.5 = (f32[8,1024]{1,0:T(8,128)S(1)}, f32[8,1024]{1,0:T(8,128)}, u32[]{:S(2)}) copy-start(f32[8,1024]{1,0:T(8,128)} %scale.1) | copy-start | bytes 98308
  47.5 58.8 %copy-start.6 = (f32[8,1024]{1,0:T(8,128)S(1)}, f32[8,1024]{1,0:T(8,128)}, u32[]{:S(2)}) copy-start(f32[8,1024]{1,0:T(8,128)} %shift.1) | copy-start | bytes 98308
  47.5 58.8 %copy-start.7 = (f32[1024]{0:T(1024)S(1)}, f32[1024]{0:T(1024)}, u32[]{:S(2)}) copy-start(f32[1024]{0:T(1024)} %param.16) | copy-start | bytes 12292
  47.5 14.2 %collective-permute-start.3 = (bf16[512,128]{1,0:T(8,128)(2,1)S(1)}, bf16[512,128]{1,0:T(8,128)(2,1)S(1)}, u32[]{:S(2)}, u32[]{:S(2)}) collective-permute-start(bf16[512,128]{1,0:T(8,128)(2,1)S(1)} %get-tuple-element.18.k0), channel_id=1, source_target_pairs={{0,48},{8,56},{16,0},{24,8},{32,16},{40,24},{48,32},{56,40},{64,11... | collective-permute-start | bytes 393224 | tf_op jit(solution)/shard_map/ppermute | solution.py:366
  48.0 13.7 %collective-permute-start.2 = (bf16[512,128]{1,0:T(8,128)(2,1)S(1)}, bf16[512,128]{1,0:T(8,128)(2,1)S(1)}, u32[]{:S(2)}, u32[]{:S(2)}) collective-permute-start(bf16[512,128]{1,0:T(8,128)(2,1)S(1)} %get-tuple-element.18.k0), channel_id=1, source_target_pairs={{0,16},{8,24},{16,32},{24,40},{32,48},{40,56},{48,0},{56,8},{64,80... | collective-permute-start | bytes 393224 | tf_op jit(solution)/shard_map/ppermute | solution.py:366
  49.5 12.2 %collective-permute-start.1 = (bf16[512,128]{1,0:T(8,128)(2,1)S(1)}, bf16[512,128]{1,0:T(8,128)(2,1)S(1)}, u32[]{:S(2)}, u32[]{:S(2)}) collective-permute-start(bf16[512,128]{1,0:T(8,128)(2,1)S(1)} %get-tuple-element.18.k0), channel_id=1, source_target_pairs={{0,32},{8,40},{16,48},{24,56},{32,0},{40,8},{48,16},{56,24},{64,96... | collective-permute-start | bytes 393224 | tf_op jit(solution)/shard_map/ppermute | solution.py:366
  52.9 7.9 %collective-permute-start.5 = (bf16[256,128]{1,0:T(8,128)(2,1)S(1)}, bf16[256,128]{1,0:T(8,128)(2,1)S(1)}, u32[]{:S(2)}, u32[]{:S(2)}) collective-permute-start(bf16[256,128]{1,0:T(8,128)(2,1)S(1)} %get-tuple-element.19.q0), channel_id=1, source_target_pairs={{0,64},{8,72},{16,80},{24,88},{32,96},{40,104},{48,112},{56,120},{... | collective-permute-start | bytes 196616 | tf_op jit(solution)/shard_map/ppermute | solution.py:365
  52.9 8.9 %collective-permute-start.4 = (bf16[256,128]{1,0:T(8,128)(2,1)S(1)}, bf16[256,128]{1,0:T(8,128)(2,1)S(1)}, u32[]{:S(2)}, u32[]{:S(2)}) collective-permute-start(bf16[256,128]{1,0:T(8,128)(2,1)S(1)} %get-tuple-element.19.q0), channel_id=1, source_target_pairs={{0,128},{8,136},{16,144},{24,152},{32,160},{40,168},{48,176},{56,1... | collective-permute-start | bytes 196616 | tf_op jit(solution)/shard_map/ppermute | solution.py:365
  60.8 45.6 %copy-start.4 = (bf16[1024,1024]{1,0:T(8,128)(2,1)S(1)}, bf16[1024,1024]{1,0:T(8,128)(2,1)}, u32[]{:S(2)}) copy-start(bf16[1024,1024]{1,0:T(8,128)(2,1)} %w_dec.1) | copy-start | bytes 6291460
  60.8 45.6 %collective-permute-start.11 = (bf16[8,64,1024]{2,1,0:T(8,128)(2,1)S(1)}, bf16[8,64,1024]{2,1,0:T(8,128)(2,1)S(1)}, u32[]{:S(2)}, u32[]{:S(2)}) collective-permute-start(bf16[8,64,1024]{2,1,0:T(8,128)(2,1)S(1)} %all-to-all-done.2._.w_mine), channel_id=1, source_target_pairs={{0,8},{8,0},{16,24},{24,16},{32,40},{40,32},{48,56},{56,48},{64,72... | collective-permute-start | bytes 3145736 | tf_op jit(solution)/shard_map/ppermute | solution.py:373
  72.1 9.3 %collective-permute-start.7 = (bf16[80,512]{1,0:T(8,128)(2,1)S(1)}, bf16[80,512]{1,0:T(8,128)(2,1)S(1)}, u32[]{:S(2)}, u32[]{:S(2)}) collective-permute-start(bf16[80,512]{1,0:T(8,128)(2,1)S(1)} %get-tuple-element.21), channel_id=1, source_target_pairs={{0,128},{8,136},{16,144},{24,152},{32,160},{40,168},{48,176},{56,1... | collective-permute-start | bytes 245768 | tf_op jit(solution)/shard_map/ppermute | solution.py:370
  75.7 8.0 %collective-permute-start.8 = (bf16[80,512]{1,0:T(8,128)(2,1)S(1)}, bf16[80,512]{1,0:T(8,128)(2,1)S(1)}, u32[]{:S(2)}, u32[]{:S(2)}) collective-permute-start(bf16[80,512]{1,0:T(8,128)(2,1)S(1)} %get-tuple-element.22), channel_id=1, source_target_pairs={{0,192},{8,200},{16,208},{24,216},{32,224},{40,232},{48,240},{56,2... | collective-permute-start | bytes 245768 | tf_op jit(solution)/shard_map/ppermute | solution.py:370
  78.6 6.6 %collective-permute-start.9 = (bf16[80,512]{1,0:T(8,128)(2,1)S(1)}, bf16[80,512]{1,0:T(8,128)(2,1)S(1)}, u32[]{:S(2)}, u32[]{:S(2)}) collective-permute-start(bf16[80,512]{1,0:T(8,128)(2,1)S(1)} %get-tuple-element.23), channel_id=1, source_target_pairs={{0,64},{8,72},{16,80},{24,88},{32,96},{40,104},{48,112},{56,120},{... | collective-permute-start | bytes 245768 | tf_op jit(solution)/shard_map/ppermute | solution.py:370
  85.2 1.3 %collective-permute-start.10 = (bf16[64,256]{1,0:T(8,128)(2,1)S(1)}, bf16[64,256]{1,0:T(8,128)(2,1)S(1)}, u32[]{:S(2)}, u32[]{:S(2)}) collective-permute-start(bf16[64,256]{1,0:T(8,128)(2,1)S(1)} %get-tuple-element.26), channel_id=1, source_target_pairs={{0,8},{8,0},{16,24},{24,16},{32,40},{40,32},{48,56},{56,48},{64,72... | collective-permute-start | bytes 98312 | tf_op jit(solution)/shard_map/ppermute | solution.py:374
where the time goes:
time: 115 us; the launch traced here: 114 us
  blocking collectives  48 us (42%)
  Pallas kernels  26.2 us (23%)
  starting transfers between devices  25 us (22%)
  waiting for transfers between devices  14 us (12%)
    all_to_all x3, blocking collectives, exchange(): return lax.all_to_all(array, 'chan', 0, 0, tiled=True)  48 us
    pallas_call x1, Pallas kernels, attend(): pl.pallas_call(attend_kernel, in_specs=[VMEM] * 8, out_specs=(VMEM,) * 4,...  10.3 us
    ppermute x3, starting transfers between devices, body(): lax.ppermute(qt, 'space', along_z(k))  9.29 us
    pallas_call x1, Pallas kernels, pool(): pl.pallas_call(pool_kernel, grid=(peers,), in_specs=[pl.BlockSpec((count,...  7.12 us
    pallas_call x1, Pallas kernels, decode(): pl.pallas_call(decode_kernel, grid=(count // each,), in_specs=[VMEM] * 7...  7.08 us
    ppermute x3, starting transfers between devices, body(): lax.ppermute(p, 'space', along_z(-k))  6.54 us
    ppermute x3, waiting for transfers between devices, body(): lax.ppermute(p, 'space', along_z(-k))  6.52 us
    ppermute x3, starting transfers between devices, body(): lax.ppermute(kv, 'space', along_x(k))  5.36 us
  transfers between devices with their start and end apart: 13, of which 7 were waited for; matrix products, arithmetic and copies ran while one was open for 0% of the time, Pallas kernels for 9%

commit v1 on v0

v1 whole, which is shorter than its diff:
```python
import functools
import math

import jax
import jax.numpy as jnp
from jax import lax
from jax.experimental import pallas as pl
from jax.experimental.pallas import tpu as pltpu
from jax.sharding import PartitionSpec as P


D = 1024
HEADS = 16
HEAD_DIM = D // HEADS
EPS = 1e-6
LOG2E = 1.4426950408889634
Z_HI, X, CORES = 4, 4, 2
F32, BF16 = jnp.float32, jnp.bfloat16

VMEM = pl.BlockSpec(memory_space=pltpu.VMEM)
ANY = pl.BlockSpec(memory_space=pl.ANY)
PARAMS = pltpu.CompilerParams(vmem_limit_bytes=24 << 20)


def cost(flops, moved):
    return pl.CostEstimate(flops=flops, bytes_accessed=moved, transcendentals=0)


def shape(dims, dtype):
    return jax.ShapeDtypeStruct(dims, dtype)


def in_three(value):
    high = value.astype(BF16)
    rest = value - high.astype(F32)
    mid = rest.astype(BF16)
    low = (rest - mid.astype(F32)).astype(BF16)
    return high.astype(F32), mid.astype(F32), low.astype(F32)


def pool_kernel(patches, var_embed, query, out):
    count = patches.shape[0]
    parts, rows, _ = out.shape
    scaled = query[...] * (LOG2E / math.sqrt(D))
    shared = jnp.sum(var_embed[...] * scaled, -1, keepdims=True)
    lane = lax.broadcasted_iota(jnp.int32, (rows, 128), 1)
    for part in range(parts):
        here = slice(part * rows, (part + 1) * rows)
        logits = [
            jnp.sum(patches[v, here].astype(F32) * scaled, -1, keepdims=True) + shared[v : v + 1, :]
            for v in range(count)
        ]
        top = functools.reduce(jnp.maximum, logits)
        expo = [jnp.exp2(l - top) for l in logits]
        total = functools.reduce(jnp.add, expo)
        inverse = 1.0 / total
        acc = jnp.zeros((rows, D), F32)
        for v in range(count):
            embedded = patches[v, here].astype(F32) + var_embed[v : v + 1, :]
            acc = acc + (expo[v] * inverse) * embedded
        out[part, :, :D] = acc.astype(BF16)
        high, mid, low = in_three(top + jnp.log2(total))
        packed = jnp.where(lane == 0, high, jnp.where(lane == 1, mid, jnp.where(lane == 2, low, 0.0)))
        out[part, :, D:] = packed.astype(BF16)


def pool(patches, var_embed, query, peers):
    count, rows, _ = patches.shape
    part = rows // peers
    each = peers // 2
    return pl.pallas_call(
        pool_kernel,
        grid=(peers // each,),
        in_specs=[
            pl.BlockSpec((count, each * part, D), lambda i: (0, i, 0)),
            pl.BlockSpec((count, D), lambda i: (0, 0)),
            pl.BlockSpec((1, D), lambda i: (0, 0)),
        ],
        out_specs=pl.BlockSpec((each, part, D + 128), lambda i: (i, 0, 0)),
        out_shape=shape((peers, part, D + 128), BF16),
        cost_estimate=cost(16 << 20, 8 << 20),
        name="pool",
    )(patches, var_embed, query)


def merge_pool_kernel(parts, pos, resid):
    peers, rows, _ = parts.shape
    logs = [jnp.sum(parts[i, :, D:].astype(F32), -1, keepdims=True) for i in range(peers)]
    top = functools.reduce(jnp.maximum, logs)
    weights = [jnp.exp2(l - top) for l in logs]
    total = functools.reduce(jnp.add, weights)
    acc = jnp.zeros((rows, D), F32)
    for i in range(peers):
        acc = acc + (weights[i] / total) * parts[i, :, :D].astype(F32)
    start = pl.multiple_of(lax.axis_index("chan") * rows, rows)
    value = (acc + pos[pl.ds(start, rows), :].astype(F32)).astype(BF16)
    for i in range(peers):
        resid[i] = value


def merge_pool(parts, pos):
    peers, rows, _ = parts.shape
    return pl.pallas_call(
        merge_pool_kernel,
        in_specs=[VMEM, VMEM],
        out_specs=VMEM,
        out_shape=shape((peers, rows, D), BF16),
        compiler_params=PARAMS,
        cost_estimate=cost(4<< 20, 2<< 20),
        name="merge_pool",
    )(parts, pos)


def project_kernel(resid, gain, weight, w_out, mine, other, copies, sems):
    share = w_out.shape[0] // CORES
    start = pl.multiple_of(lax.axis_index("space") % CORES * share, share)
    source = w_out.at[pl.ds(start, share), :]
    moved = [pltpu.make_async_copy(source, copies.at[i], sems.at[i]) for i in range(copies.shape[0])]
    for copy in moved:
        copy.start()
    half = resid.shape[0] // 2
    value = resid[...].astype(F32)
    mean = jnp.mean(value * value, -1, keepdims=True)
    x = (value * lax.rsqrt(mean + EPS) * gain[...]).astype(BF16)
    q, k, v = (jnp.dot(x, weight[i], preferred_element_type=F32) for i in range(3))
    low = lax.broadcasted_iota(jnp.int32, (half, 2 * HEAD_DIM), 1) < HEAD_DIM
    upper, lower = k[:half], k[half:]
    keys = (
        jnp.where(low, upper, pltpu.roll(lower, HEAD_DIM, 1)),
        jnp.where(low, pltpu.roll(upper, HEAD_DIM, 1), lower),
    )
    turned = [(q * (1.0 / math.sqrt(HEAD_DIM))).T, v.T]
    queries, values = ((t[:HEAD_DIM], t[HEAD_DIM:]) for t in turned)
    is_first = lax.axis_index("space") % CORES == 0
    for ref, (a, b) in ((mine, (0, 1)), (other, (1, 0))):
        key, value, query = (
            jnp.where(is_first, pair[a], pair[b]).astype(BF16) for pair in (keys, values, queries)
        )
        ref[:half, :] = key
        for i, turn in ((1, value), (2, query)):
            ref[i * half : i * half + HEAD_DIM, :] = turn[:, :half]
            ref[i * half + HEAD_DIM : (i + 1) * half, :] = turn[:, half:]
    for copy in moved:
        copy.wait()


def project(resid, gain, weight, w_out, peers):
    out = shape((resid.shape[0] + 2 * HEAD_DIM, 128), BF16)
    return pl.pallas_call(
        project_kernel,
        in_specs=[VMEM] * 4,
        out_specs=(VMEM, VMEM, ANY),
        out_shape=(out, out, shape((peers, w_out.shape[0] // CORES, D), BF16)),
        scratch_shapes=[pltpu.SemaphoreType.DMA((peers,))],
        compiler_params=PARAMS,
        cost_estimate=cost(200 << 20, 4<< 20),
        name="project",
    )(resid, gain, weight, w_out)


def pair_kernel(mine, swapped, kv, qt):
    rows, turned = kv.shape[0] // 2, qt.shape[0] // 2
    kv[:rows, :] = mine[:rows, :]
    kv[rows:, :] = swapped[:rows, :]
    qt[:turned, :] = mine[rows:, :]
    qt[turned:, :] = swapped[rows:, :]


def pair(mine, swapped):
    rows = mine.shape[0] - 2 * HEAD_DIM
    return pl.pallas_call(
        pair_kernel,
        in_specs=[VMEM, VMEM],
        out_specs=(VMEM, VMEM),
        out_shape=(shape((2 * rows, 128), BF16), shape((4 * HEAD_DIM, 128), BF16)),
        compiler_params=PARAMS,
        cost_estimate=cost(1<< 20, 1<< 20),
        name="pair",
    )(mine, swapped)


def attend_kernel(k0, k1, k2, k3, queries, out):
    zeros = jnp.zeros((HEAD_DIM, 256), BF16)
    groups = ((k0, k1), (k2, k3))

    def scores_of(tile, refs):
        at = tile * 2 * HEAD_DIM
        turned = jnp.concatenate(
            [queries[at : at + HEAD_DIM, :], queries[at + HEAD_DIM : at + 2 * HEAD_DIM, :]], 1
        )
        sides = jnp.concatenate([turned, zeros], 0), jnp.concatenate([zeros, turned], 0)
        return [
            jnp.dot(ref[at : at + 128, :], side, preferred_element_type=F32)
            for ref in refs
            for at in (0, 256)
            for side in sides
        ]

    def merged(state, scores, refs):
        top = functools.reduce(jnp.maximum, [jnp.max(s, 0, keepdims=True) for s in scores]) * LOG2E
        if state is not None:
            top = jnp.maximum(state[0], top)
        probs = [jnp.exp2(s * LOG2E - top) for s in scores]
        total = functools.reduce(jnp.add, [jnp.sum(p, 0, keepdims=True) for p in probs])
        values = [
            jnp.concatenate([ref[at + 128 : at + 192, :], ref[at + 192 : at + 256, :]], 1)
            for ref in refs
            for at in (0, 256)
        ]
        acc = jnp.zeros((HEAD_DIM, 256), F32)
        for i, value in enumerate(values):
            pair = jnp.concatenate([p.astype(BF16) for p in probs[2 * i : 2 * i + 2]], 0)
            acc += jnp.dot(value, pair, preferred_element_type=F32)
        if state is not None:
            rescale = jnp.exp2(state[0] - top)
            total = total + rescale * state[1]
            acc = acc + rescale * state[2]
        return top, total, acc

    work = [(tile, refs) for refs in groups for tile in range(2)]
    states = [None, None]
    ahead = scores_of(*work[0])
    for i, (tile, refs) in enumerate(work):
        scores = ahead
        if i + 1 < len(work):
            ahead = scores_of(*work[i + 1])
        states[tile] = merged(states[tile], scores, refs)
    for tile, (top, total, acc) in enumerate(states):
        lanes = slice(tile * 256, tile * 256 + 256)
        out[:HEAD_DIM, lanes] = (acc / total).astype(BF16)
        high, mid, low = in_three(top + jnp.log2(total))
        row = lax.broadcasted_iota(jnp.int32, (16, 256), 0)
        logs = jnp.where(row == 0, high, jnp.where(row == 1, mid, jnp.where(row == 2, low, 0.0)))
        out[HEAD_DIM:, lanes] = logs.astype(BF16)


def attend(key_pieces, queries):
    each = key_pieces[0].shape[0]
    return pl.pallas_call(
        attend_kernel,
        in_specs=[VMEM] * 5,
        out_specs=VMEM,
        out_shape=shape((HEAD_DIM + 16, each), BF16),
        compiler_params=PARAMS,
        cost_estimate=cost(1 << 30, 2 << 20),
        name="attend",
    )(*key_pieces, queries)


def merge_heads_kernel(p0, p1, p2, p3, mine, other):
    refs = (p0, p1, p2, p3)
    logs = [jnp.sum(r[HEAD_DIM:, :].astype(F32), 0, keepdims=True) for r in refs]
    top = functools.reduce(jnp.maximum, logs)
    weights = [jnp.exp2(l - top) for l in logs]
    total = functools.reduce(jnp.add, weights)
    acc = jnp.zeros((HEAD_DIM, p0.shape[1]), F32)
    for r, w in zip(refs, weights):
        acc = acc + (w / total) * r[:HEAD_DIM, :].astype(F32)
    half = p0.shape[1] // 2
    mine[...] = acc[:, :half].astype(BF16)
    other[...] = acc[:, half:].astype(BF16)


def merge_heads(parts):
    width = parts[0].shape[1] // 2
    out = shape((HEAD_DIM, width), BF16)
    return pl.pallas_call(
        merge_heads_kernel,
        in_specs=[VMEM] * 4,
        out_specs=(VMEM, VMEM),
        out_shape=(out, out),
        compiler_params=PARAMS,
        cost_estimate=cost(1<< 20, 1<< 20),
        name="merge_heads",
    )(*parts)


def spread_kernel(mine, other, _, out):
    both = jnp.concatenate([mine[...].astype(F32), other[...].astype(F32)], 0)
    value = both.T.astype(BF16)
    for i in range(out.shape[0]):
        out[i] = value


def spread(mine, other, after, peers):
    return pl.pallas_call(
        spread_kernel,
        in_specs=[VMEM, VMEM, ANY],
        out_specs=VMEM,
        out_shape=shape((peers, mine.shape[1], 2 * HEAD_DIM), BF16),
        compiler_params=PARAMS,
        cost_estimate=cost(1<< 20, 1<< 20),
        name="spread",
    )(mine, other, after)


def trunk_kernel(mixed, w_mine, w_other, resid, gain, normed):
    heads = jnp.concatenate([mixed[i] for i in range(mixed.shape[0])], 1)
    weights = [ref[i] for i in range(mixed.shape[0]) for ref in (w_mine, w_other)]
    value = jnp.dot(heads, jnp.concatenate(weights, 0), preferred_element_type=F32)
    value = value + resid[...].astype(F32)
    mean = jnp.mean(value * value, -1, keepdims=True)
    normed[...] = (value * lax.rsqrt(mean + EPS) * gain[...]).astype(BF16)


def trunk(mixed, w_mine, w_other, resid, gain):
    return pl.pallas_call(
        trunk_kernel,
        in_specs=[VMEM] * 5,
        out_specs=VMEM,
        out_shape=shape(resid.shape, BF16),
        compiler_params=PARAMS,
        cost_estimate=cost(1 << 30, 4 << 20),
        name="trunk",
    )(mixed, w_mine, w_other, resid, gain)


def decode_kernel(normed, scale, shift, weight, out):
    each = out.shape[0]
    parts = []
    for i in range(each):
        v = pl.program_id(0) * each + i
        row = (1.0 + scale[pl.ds(v, 1), :], shift[pl.ds(v, 1), :])
        parts.append((normed[...].astype(F32) * row[0] + row[1]).astype(BF16))
    modulated = jnp.concatenate(parts, 0)
    result = jnp.dot(modulated, weight[...], preferred_element_type=F32).astype(BF16)
    out[...] = result.reshape(out.shape)


def decode(normed, scale, shift, weight):
    count, rows = scale.shape[0], normed.shape[0]
    each = 2
    return pl.pallas_call(
        decode_kernel,
        grid=(count // each,),
        in_specs=[VMEM] * 4,
        out_specs=pl.BlockSpec((each, rows, D), lambda v: (v, 0, 0)),
        out_shape=shape((count, rows, D), BF16),
        compiler_params=PARAMS,
        cost_estimate=cost(5 << 30, 8 << 20),
        name="decode",
    )(normed, scale, shift, weight)


def space_index(z, x, core):
    return (z * X + x) * CORES + core


def moves(step):
    return [
        (space_index(z, x, c), space_index(*step(z, x, c)))
        for z in range(Z_HI)
        for x in range(X)
        for c in range(CORES)
    ]


SWAP = moves(lambda z, x, c: (z, x, 1 - c))


def along_x(k):
    return moves(lambda z, x, c: (z, (x + k) % X, c))


def along_z(k):
    return moves(lambda z, x, c: ((z + k) % Z_HI, x, c))


def exchange(array):
    return lax.all_to_all(array, "chan", 0, 0, tiled=True)


def body(
    patches,
    var_embed,
    agg_query,
    pos_embed,
    gain_first,
    gain_second,
    w_qkv,
    w_out,
    w_dec,
    mod_scale,
    mod_shift,
):
    rows = patches.shape[1]
    peers = lax.axis_size("chan")

    parts = exchange(pool(patches, var_embed, agg_query.reshape(1, D), peers))
    resid = exchange(merge_pool(parts, pos_embed)).reshape(rows, D)

    mine, other, copies = project(
        resid, gain_first.reshape(1, D), w_qkv.transpose(1, 0, 2), w_out, peers
    )
    kv, qt = pair(mine, lax.ppermute(other, "space", SWAP))
    key_pieces = [kv] + [lax.ppermute(kv, "space", along_z(k)) for k in (2, 1, 3)]
    query_pieces = [lax.ppermute(qt, "space", along_x(k)) for k in (2, 1, 3)]
    w_mine = exchange(copies)
    back = []
    for k, piece in zip((2, 1, 3), query_pieces):
        partial = attend(key_pieces, piece)
        back.append(lax.ppermute(partial, "space", along_x(-k)))
    back.append(attend(key_pieces, qt))
    mine, other = merge_heads(back)
    w_other = lax.ppermute(w_mine, "space", SWAP)
    mixed = exchange(spread(mine, lax.ppermute(other, "space", SWAP), w_mine, peers))
    normed = trunk(mixed, w_mine, w_other, resid, gain_second.reshape(1, D))
    return decode(normed, mod_scale, mod_shift, w_dec)


def solution(mesh):
    placed = (
        P("chan", "space", None),
        P("chan", None),
        P(),
        P("space", None),
        P(),
        P(),
        P(None, None, "chan"),
        P("chan", None),
        P(),
        P("chan", None),
        P("chan", None),
    )

    return jax.shard_map(
        body, mesh=mesh, in_specs=placed, out_specs=P("chan", "space", None), check_vma=False
    )
```

time: 115 us -> 103 us (0.90)
  Pallas kernels: 26.2 us -> 20 us
  blocking collectives: 48 us -> 43.9 us
  starting transfers between devices: 25 us -> 22.7 us
    pallas_call x6 -> x10, Pallas kernels: 26 us -> 19.7 us  [the longest x4 6.3 us: attend(): pl.pallas_call(attend_kernel, in_specs=[VMEM] * 5, out_specs=VMEM, out_sh...]
    all_to_all x3, blocking collectives: 48 us -> 43.9 us  [exchange(): return lax.all_to_all(array, 'chan', 0, 0, tiled=True)]
    ppermute x10, starting transfers between devices: 21.3 us -> 19 us  [the longest x3 9.29 us: body(): lax.ppermute(kv, 'space', along_z(k))]
  transfers between devices with their start and end apart: 13 -> 13, of which waited for: 7 -> 6; matrix products, arithmetic and copies ran while one was open for 0% -> 0% of each run, Pallas kernels for 9% -> 6%
where the time goes in v1:
time: 103 us; the launch traced here: 102 us
  blocking collectives  43.9 us (43%)
  starting transfers between devices  22.7 us (22%)
  Pallas kernels  20 us (19%)
  waiting for transfers between devices  14.9 us (14%)
    all_to_all x3, blocking collectives, exchange(): return lax.all_to_all(array, 'chan', 0, 0, tiled=True)  43.9 us
    ppermute x3, starting transfers between devices, body(): lax.ppermute(kv, 'space', along_z(k))  9.29 us
    ppermute x3, waiting for transfers between devices, body(): lax.ppermute(kv, 'space', along_z(k))  8 us
    pallas_call x4, Pallas kernels, attend(): pl.pallas_call(attend_kernel, in_specs=[VMEM] * 5, out_specs=VMEM, out_sh...  6.3 us
    pallas_call x1, Pallas kernels, decode(): pl.pallas_call(decode_kernel, grid=(count // each,), in_specs=[VMEM] * 4,...  6.1 us
    ppermute x3, starting transfers between devices, body(): query_pieces = [lax.ppermute(qt, 'space', along_x(k)) for k in (2, 1, 3)]  5.04 us
    pallas_call x1, Pallas kernels, pool(): pl.pallas_call(pool_kernel, grid=(peers // each,), in_specs=[pl.BlockSpec...  4.66 us
    ppermute x3, starting transfers between devices, body(): back.append(lax.ppermute(partial, 'space', along_x(-k)))  4.58 us
  transfers between devices with their start and end apart: 13, of which 6 were waited for; matrix products, arithmetic and copies ran while one was open for 0% of the time, Pallas kernels for 6%

profile of v1, /device:TPU:2, one launch (start us, length us, event | category | flops | bytes accessed | tf_op | source)
XLA Modules:
  0.0 101.7 jit_solution(1588758768919074858)
XLA Ops:
  0.0 0.0 copy-start.1
  0.0 0.0 copy-start
  0.0 0.0 copy-start.2
  0.0 0.0 copy-start.3
  0.0 4.7 %pool.1 = bf16[8,32,1152]{2,1,0:T(8,128)(2,1)} custom-call(bf16[8,256,1024]{2,1,0:T(8,128)(2,1)} %patches.1, f32[8,1024]{1,0:T(8,128)} %var_embed.1, f32[1,1024]{1,0:T(1,128)} %bitcast.10), custom_call_target="tpu_custom_call" | custom-call | flops 16777216 | bytes 8388608 | tf_op jit(solution)/shard_map/pool/pallas_call | solution.py:71
  4.7 16.7 %all_to_all.20.parts = bf16[8,32,1152]{2,1,0:T(8,128)(2,1)S(1)} all-to-all(bf16[8,32,1152]{2,1,0:T(8,128)(2,1)} %pool.1), channel_id=1, replica_groups=mesh['space'=32,'chan'=8] {'chan'}, dimensions={0} | all-to-all | bytes 1179648 | tf_op jit(solution)/shard_map/all_to_all | solution.py:370
  21.4 0.0 copy-done.1
  21.4 0.3 merge_pool.1
  21.7 11.6 %all_to_all.21 = bf16[8,32,1024]{2,1,0:T(8,128)(2,1)S(1)} all-to-all(bf16[8,32,1024]{2,1,0:T(8,128)(2,1)S(1)} %merge_pool.1), channel_id=1, replica_groups=mesh['space'=32,'chan'=8] {'chan'}, dimensions={0} | all-to-all | bytes 1048576 | tf_op jit(solution)/shard_map/all_to_all | solution.py:370
  33.3 0.0 copy-done
  33.3 0.0 copy-done.2
  33.3 0.0 copy-done.3
  33.3 1.6 %project.1 = (bf16[384,128]{1,0:T(8,128)(2,1)S(1)}, bf16[384,128]{1,0:T(8,128)(2,1)S(1)}, bf16[8,64,1024]{2,1,0:T(8,128)(2,1)}) custom-call(bf16[256,1024]{1,0:T(8,128)(2,1)S(1)} %bitcast.5, f32[1,1024]{1,0:T(1,128)S(1)} %bitcast.8, bf16[3,1024,128]{2,1,0:T(8,128)(2,1)S(1)} %bitcast.7, bf16[128,1024]{1,0:T(8,128)(2,1)S(1)} %copy-done.2), custom_call_target="tpu_custom_call" | custom-call | flops 209715200 | bytes 4194304 | tf_op jit(solution)/shard_map/project/pallas_call | solution.py:149
  34.9 3.6 %all-to-all-start.2 = ((bf16[8,64,1024]{2,1,0:T(8,128)(2,1)}), bf16[8,64,1024]{2,1,0:T(8,128)(2,1)S(1)}, u32[]{:S(2)}, u32[]{:S(2)}) async-start(bf16[8,64,1024]{2,1,0:T(8,128)(2,1)} %get-tuple-element.18), calls=%async_computation.2 | async-start | bytes 2097152 | tf_op jit(solution)/shard_map/all_to_all | solution.py:370
  38.5 0.1 collective-permute-start
  38.6 1.3 %collective-permute-done.swapped = bf16[384,128]{1,0:T(8,128)(2,1)S(1)} collective-permute-done((bf16[384,128]{1,0:T(8,128)(2,1)S(1)}, bf16[384,128]{1,0:T(8,128)(2,1)S(1)}, u32[]{:S(2)}, u32[]{:S(2)}) %collective-permute-start) | collective-permute-done | bytes 98336 | tf_op jit(solution)/shard_map/ppermute | solution.py:395
  39.9 5.5 %collective-permute-start.3 = (bf16[512,128]{1,0:T(8,128)(2,1)S(1)}, bf16[512,128]{1,0:T(8,128)(2,1)S(1)}, u32[]{:S(2)}, u32[]{:S(2)}) collective-permute-start(bf16[512,128]{1,0:T(8,128)(2,1)S(1)} %get-tuple-element.14.k0), channel_id=1, source_target_pairs={{0,192},{8,200},{16,208},{24,216},{32,224},{40,232},{48,240},{56,2... | collective-permute-start | bytes 393224 | tf_op jit(solution)/shard_map/ppermute | solution.py:396
  45.4 0.0 collective-permute-start.2
  45.4 3.8 %collective-permute-start.1 = (bf16[512,128]{1,0:T(8,128)(2,1)S(1)}, bf16[512,128]{1,0:T(8,128)(2,1)S(1)}, u32[]{:S(2)}, u32[]{:S(2)}) collective-permute-start(bf16[512,128]{1,0:T(8,128)(2,1)S(1)} %get-tuple-element.14.k0), channel_id=1, source_target_pairs={{0,128},{8,136},{16,144},{24,152},{32,160},{40,168},{48,176},{56,1... | collective-permute-start | bytes 393224 | tf_op jit(solution)/shard_map/ppermute | solution.py:396
  49.2 2.1 %collective-permute-start.4 = (bf16[256,128]{1,0:T(8,128)(2,1)S(1)}, bf16[256,128]{1,0:T(8,128)(2,1)S(1)}, u32[]{:S(2)}, u32[]{:S(2)}) collective-permute-start(bf16[256,128]{1,0:T(8,128)(2,1)S(1)} %get-tuple-element.15.queries), channel_id=1, source_target_pairs={{0,32},{8,40},{16,48},{24,56},{32,0},{40,8},{48,16},{56,24},{64,96... | collective-permute-start | bytes 196616 | tf_op jit(solution)/shard_map/ppermute | solution.py:397
  51.3 1.4 %collective-permute-start.8 = (bf16[256,128]{1,0:T(8,128)(2,1)S(1)}, bf16[256,128]{1,0:T(8,128)(2,1)S(1)}, u32[]{:S(2)}, u32[]{:S(2)}) collective-permute-start(bf16[256,128]{1,0:T(8,128)(2,1)S(1)} %get-tuple-element.15.queries), channel_id=1, source_target_pairs={{0,48},{8,56},{16,0},{24,8},{32,16},{40,24},{48,32},{56,40},{64,11... | collective-permute-start | bytes 196616 | tf_op jit(solution)/shard_map/ppermute | solution.py:397
  52.7 2.2 %collective-permute-done.4.queries = bf16[256,128]{1,0:T(8,128)(2,1)S(1)} collective-permute-done((bf16[256,128]{1,0:T(8,128)(2,1)S(1)}, bf16[256,128]{1,0:T(8,128)(2,1)S(1)}, u32[]{:S(2)}, u32[]{:S(2)}) %collective-permute-start.4) | collective-permute-done | bytes 65568 | tf_op jit(solution)/shard_map/ppermute | solution.py:397
  55.0 1.5 %collective-permute-start.6 = (bf16[256,128]{1,0:T(8,128)(2,1)S(1)}, bf16[256,128]{1,0:T(8,128)(2,1)S(1)}, u32[]{:S(2)}, u32[]{:S(2)}) collective-permute-start(bf16[256,128]{1,0:T(8,128)(2,1)S(1)} %get-tuple-element.15.queries), channel_id=1, source_target_pairs={{0,16},{8,24},{16,32},{24,40},{32,48},{40,56},{48,0},{56,8},{64,80... | collective-permute-start | bytes 196616 | tf_op jit(solution)/shard_map/ppermute | solution.py:397
  56.4 0.0 collective-permute-done.3.k3
  56.4 5.6 %collective-permute-done.2.k2 = bf16[512,128]{1,0:T(8,128)(2,1)S(1)} collective-permute-done((bf16[512,128]{1,0:T(8,128)(2,1)S(1)}, bf16[512,128]{1,0:T(8,128)(2,1)S(1)}, u32[]{:S(2)}, u32[]{:S(2)}) %collective-permute-start.2) | collective-permute-done | bytes 131104 | tf_op jit(solution)/shard_map/ppermute | solution.py:396
  62.1 2.4 %collective-permute-done.1.k1 = bf16[512,128]{1,0:T(8,128)(2,1)S(1)} collective-permute-done((bf16[512,128]{1,0:T(8,128)(2,1)S(1)}, bf16[512,128]{1,0:T(8,128)(2,1)S(1)}, u32[]{:S(2)}, u32[]{:S(2)}) %collective-permute-start.1) | collective-permute-done | bytes 131104 | tf_op jit(solution)/shard_map/ppermute | solution.py:396
  64.4 1.6 %attend.4 = bf16[80,512]{1,0:T(8,128)(2,1)S(1)} custom-call(bf16[512,128]{1,0:T(8,128)(2,1)S(1)} %get-tuple-element.14.k0, bf16[512,128]{1,0:T(8,128)(2,1)S(1)} %collective-permute-done.1.k1, bf16[512,128]{1,0:T(8,128)(2,1)S(1)} %collective-permute-done.2.k2, bf16[512,128]{1,0:T(8,128)(2,1)S(1)} %collective-permute-done.3.k3, ...), custom_call_target="tpu_custom_call" | custom-call | flops 1073741824 | bytes 2097152 | tf_op jit(solution)/shard_map/attend/pallas_call | solution.py:239
  66.0 2.2 %collective-permute-start.5 = (bf16[80,512]{1,0:T(8,128)(2,1)S(1)}, bf16[80,512]{1,0:T(8,128)(2,1)S(1)}, u32[]{:S(2)}, u32[]{:S(2)}) collective-permute-start(bf16[80,512]{1,0:T(8,128)(2,1)S(1)} %attend.4), channel_id=1, source_target_pairs={{0,32},{8,40},{16,48},{24,56},{32,0},{40,8},{48,16},{56,24},{64,96... | collective-permute-start | bytes 245768 | tf_op jit(solution)/shard_map/ppermute | solution.py:402
  68.2 0.0 collective-permute-done.6.queries
  68.2 1.6 %attend.5 = bf16[80,512]{1,0:T(8,128)(2,1)S(1)} custom-call(bf16[512,128]{1,0:T(8,128)(2,1)S(1)} %get-tuple-element.14.k0, bf16[512,128]{1,0:T(8,128)(2,1)S(1)} %collective-permute-done.1.k1, bf16[512,128]{1,0:T(8,128)(2,1)S(1)} %collective-permute-done.2.k2, bf16[512,128]{1,0:T(8,128)(2,1)S(1)} %collective-permute-done.3.k3, ...), custom_call_target="tpu_custom_call" | custom-call | flops 1073741824 | bytes 2097152 | tf_op jit(solution)/shard_map/attend/pallas_call | solution.py:239
  69.8 1.7 %collective-permute-start.7 = (bf16[80,512]{1,0:T(8,128)(2,1)S(1)}, bf16[80,512]{1,0:T(8,128)(2,1)S(1)}, u32[]{:S(2)}, u32[]{:S(2)}) collective-permute-start(bf16[80,512]{1,0:T(8,128)(2,1)S(1)} %attend.5), channel_id=1, source_target_pairs={{0,48},{8,56},{16,0},{24,8},{32,16},{40,24},{48,32},{56,40},{64,11... | collective-permute-start | bytes 245768 | tf_op jit(solution)/shard_map/ppermute | solution.py:402
  71.5 0.0 collective-permute-done.8.queries
  71.5 1.6 %attend.6 = bf16[80,512]{1,0:T(8,128)(2,1)S(1)} custom-call(bf16[512,128]{1,0:T(8,128)(2,1)S(1)} %get-tuple-element.14.k0, bf16[512,128]{1,0:T(8,128)(2,1)S(1)} %collective-permute-done.1.k1, bf16[512,128]{1,0:T(8,128)(2,1)S(1)} %collective-permute-done.2.k2, bf16[512,128]{1,0:T(8,128)(2,1)S(1)} %collective-permute-done.3.k3, ...), custom_call_target="tpu_custom_call" | custom-call | flops 1073741824 | bytes 2097152 | tf_op jit(solution)/shard_map/attend/pallas_call | solution.py:239
  73.1 0.0 copy-start.7
  73.1 0.7 collective-permute-start.9
  73.8 0.0 all-to-all-done.2._.w_mine
  73.8 0.0 collective-permute-start.11
  73.8 1.6 %attend.7.p3 = bf16[80,512]{1,0:T(8,128)(2,1)S(1)} custom-call(bf16[512,128]{1,0:T(8,128)(2,1)S(1)} %get-tuple-element.14.k0, bf16[512,128]{1,0:T(8,128)(2,1)S(1)} %collective-permute-done.1.k1, bf16[512,128]{1,0:T(8,128)(2,1)S(1)} %collective-permute-done.2.k2, bf16[512,128]{1,0:T(8,128)(2,1)S(1)} %collective-permute-done.3.k3, ...), custom_call_target="tpu_custom_call" | custom-call | flops 1073741824 | bytes 2097152 | tf_op jit(solution)/shard_map/attend/pallas_call | solution.py:239
  75.4 0.0 copy-start.4
  75.4 0.0 copy-start.5
  75.4 0.0 copy-start.6
  75.4 0.0 collective-permute-done.5.p0
  75.4 0.0 collective-permute-done.7.p1
  75.4 2.2 %collective-permute-done.9.p2 = bf16[80,512]{1,0:T(8,128)(2,1)S(1)} collective-permute-done((bf16[80,512]{1,0:T(8,128)(2,1)S(1)}, bf16[80,512]{1,0:T(8,128)(2,1)S(1)}, u32[]{:S(2)}, u32[]{:S(2)}) %collective-permute-start.9) | collective-permute-done | bytes 81952 | tf_op jit(solution)/shard_map/ppermute | solution.py:402
  77.6 0.1 merge_heads.1
  77.7 0.1 collective-permute-start.10
  77.8 1.2 %collective-permute-done.10.other = bf16[64,256]{1,0:T(8,128)(2,1)S(1)} collective-permute-done((bf16[64,256]{1,0:T(8,128)(2,1)S(1)}, bf16[64,256]{1,0:T(8,128)(2,1)S(1)}, u32[]{:S(2)}, u32[]{:S(2)}) %collective-permute-start.10) | collective-permute-done | bytes 32800 | tf_op jit(solution)/shard_map/ppermute | solution.py:406
  79.0 0.1 spread.1
  79.2 15.5 %all_to_all.22.mixed = bf16[8,256,128]{2,1,0:T(8,128)(2,1)S(1)} all-to-all(bf16[8,256,128]{2,1,0:T(8,128)(2,1)S(1)} %spread.1), channel_id=1, replica_groups=mesh['space'=32,'chan'=8] {'chan'}, dimensions={0} | all-to-all | bytes 1048576 | tf_op jit(solution)/shard_map/all_to_all | solution.py:370
  94.7 0.0 collective-permute-done.11.w_other
  94.7 0.0 copy-done.7
  94.7 0.9 trunk.1.normed
  95.5 0.0 copy-done.4
  95.5 0.0 copy-done.5
  95.6 0.0 copy-done.6
  95.6 6.1 %decode.1 = bf16[8,256,1024]{2,1,0:T(8,128)(2,1)} custom-call(bf16[256,1024]{1,0:T(8,128)(2,1)S(1)} %trunk.1.normed, f32[8,1024]{1,0:T(8,128)S(1)} %copy-done.5, f32[8,1024]{1,0:T(8,128)S(1)} %copy-done.6, bf16[1024,1024]{1,0:T(8,128)(2,1)S(1)} %copy-done.4), custom_call_target="tpu_custom_call" | custom-call | flops 5368709120 | bytes 8388608 | tf_op jit(solution)/shard_map/decode/pallas_call | solution.py:333
  (1 shorter events, 0.0 us)
Async XLA Ops:
  0.0 21.4 %copy-start.1 = (bf16[256,1024]{1,0:T(8,128)(2,1)S(1)}, bf16[256,1024]{1,0:T(8,128)(2,1)}, u32[]{:S(2)}) copy-start(bf16[256,1024]{1,0:T(8,128)(2,1)} %pos.1) | copy-start | bytes 1572868
  0.0 33.3 %copy-start = (bf16[1024,3,128]{2,0,1:T(8,128)(2,1)S(1)}, bf16[1024,3,128]{2,0,1:T(8,128)(2,1)}, u32[]{:S(2)}) copy-start(bf16[1024,3,128]{2,0,1:T(8,128)(2,1)} %param.17) | copy-start | bytes 2359300
  0.0 33.3 %copy-start.2 = (bf16[128,1024]{1,0:T(8,128)(2,1)S(1)}, bf16[128,1024]{1,0:T(8,128)(2,1)}, u32[]{:S(2)}) copy-start(bf16[128,1024]{1,0:T(8,128)(2,1)} %w_out.1) | copy-start | bytes 786436
  0.0 33.3 %copy-start.3 = (f32[1024]{0:T(1024)S(1)}, f32[1024]{0:T(1024)}, u32[]{:S(2)}) copy-start(f32[1024]{0:T(1024)} %param.15) | copy-start | bytes 12292
  34.9 38.9 %all-to-all-start.2 = ((bf16[8,64,1024]{2,1,0:T(8,128)(2,1)}), bf16[8,64,1024]{2,1,0:T(8,128)(2,1)S(1)}, u32[]{:S(2)}, u32[]{:S(2)}) async-start(bf16[8,64,1024]{2,1,0:T(8,128)(2,1)} %get-tuple-element.18), calls=%async_computation.2 | async-start | bytes 2097152 | tf_op jit(solution)/shard_map/all_to_all | solution.py:370
  38.5 1.4 %collective-permute-start = (bf16[384,128]{1,0:T(8,128)(2,1)S(1)}, bf16[384,128]{1,0:T(8,128)(2,1)S(1)}, u32[]{:S(2)}, u32[]{:S(2)}) collective-permute-start(bf16[384,128]{1,0:T(8,128)(2,1)S(1)} %get-tuple-element.13), channel_id=1, source_target_pairs={{0,8},{8,0},{16,24},{24,16},{32,40},{40,32},{48,56},{56,48},{64,72... | collective-permute-start | bytes 294920 | tf_op jit(solution)/shard_map/ppermute | solution.py:395
  39.9 16.6 %collective-permute-start.3 = (bf16[512,128]{1,0:T(8,128)(2,1)S(1)}, bf16[512,128]{1,0:T(8,128)(2,1)S(1)}, u32[]{:S(2)}, u32[]{:S(2)}) collective-permute-start(bf16[512,128]{1,0:T(8,128)(2,1)S(1)} %get-tuple-element.14.k0), channel_id=1, source_target_pairs={{0,192},{8,200},{16,208},{24,216},{32,224},{40,232},{48,240},{56,2... | collective-permute-start | bytes 393224 | tf_op jit(solution)/shard_map/ppermute | solution.py:396
  45.4 16.7 %collective-permute-start.2 = (bf16[512,128]{1,0:T(8,128)(2,1)S(1)}, bf16[512,128]{1,0:T(8,128)(2,1)S(1)}, u32[]{:S(2)}, u32[]{:S(2)}) collective-permute-start(bf16[512,128]{1,0:T(8,128)(2,1)S(1)} %get-tuple-element.14.k0), channel_id=1, source_target_pairs={{0,64},{8,72},{16,80},{24,88},{32,96},{40,104},{48,112},{56,120},{... | collective-permute-start | bytes 393224 | tf_op jit(solution)/shard_map/ppermute | solution.py:396
  45.4 19.1 %collective-permute-start.1 = (bf16[512,128]{1,0:T(8,128)(2,1)S(1)}, bf16[512,128]{1,0:T(8,128)(2,1)S(1)}, u32[]{:S(2)}, u32[]{:S(2)}) collective-permute-start(bf16[512,128]{1,0:T(8,128)(2,1)S(1)} %get-tuple-element.14.k0), channel_id=1, source_target_pairs={{0,128},{8,136},{16,144},{24,152},{32,160},{40,168},{48,176},{56,1... | collective-permute-start | bytes 393224 | tf_op jit(solution)/shard_map/ppermute | solution.py:396
  49.2 5.8 %collective-permute-start.4 = (bf16[256,128]{1,0:T(8,128)(2,1)S(1)}, bf16[256,128]{1,0:T(8,128)(2,1)S(1)}, u32[]{:S(2)}, u32[]{:S(2)}) collective-permute-start(bf16[256,128]{1,0:T(8,128)(2,1)S(1)} %get-tuple-element.15.queries), channel_id=1, source_target_pairs={{0,32},{8,40},{16,48},{24,56},{32,0},{40,8},{48,16},{56,24},{64,96... | collective-permute-start | bytes 196616 | tf_op jit(solution)/shard_map/ppermute | solution.py:397
  51.3 20.2 %collective-permute-start.8 = (bf16[256,128]{1,0:T(8,128)(2,1)S(1)}, bf16[256,128]{1,0:T(8,128)(2,1)S(1)}, u32[]{:S(2)}, u32[]{:S(2)}) collective-permute-start(bf16[256,128]{1,0:T(8,128)(2,1)S(1)} %get-tuple-element.15.queries), channel_id=1, source_target_pairs={{0,48},{8,56},{16,0},{24,8},{32,16},{40,24},{48,32},{56,40},{64,11... | collective-permute-start | bytes 196616 | tf_op jit(solution)/shard_map/ppermute | solution.py:397
  55.0 13.3 %collective-permute-start.6 = (bf16[256,128]{1,0:T(8,128)(2,1)S(1)}, bf16[256,128]{1,0:T(8,128)(2,1)S(1)}, u32[]{:S(2)}, u32[]{:S(2)}) collective-permute-start(bf16[256,128]{1,0:T(8,128)(2,1)S(1)} %get-tuple-element.15.queries), channel_id=1, source_target_pairs={{0,16},{8,24},{16,32},{24,40},{32,48},{40,56},{48,0},{56,8},{64,80... | collective-permute-start | bytes 196616 | tf_op jit(solution)/shard_map/ppermute | solution.py:397
  66.0 9.4 %collective-permute-start.5 = (bf16[80,512]{1,0:T(8,128)(2,1)S(1)}, bf16[80,512]{1,0:T(8,128)(2,1)S(1)}, u32[]{:S(2)}, u32[]{:S(2)}) collective-permute-start(bf16[80,512]{1,0:T(8,128)(2,1)S(1)} %attend.4), channel_id=1, source_target_pairs={{0,32},{8,40},{16,48},{24,56},{32,0},{40,8},{48,16},{56,24},{64,96... | collective-permute-start | bytes 245768 | tf_op jit(solution)/shard_map/ppermute | solution.py:402
  69.8 5.6 %collective-permute-start.7 = (bf16[80,512]{1,0:T(8,128)(2,1)S(1)}, bf16[80,512]{1,0:T(8,128)(2,1)S(1)}, u32[]{:S(2)}, u32[]{:S(2)}) collective-permute-start(bf16[80,512]{1,0:T(8,128)(2,1)S(1)} %attend.5), channel_id=1, source_target_pairs={{0,48},{8,56},{16,0},{24,8},{32,16},{40,24},{48,32},{56,40},{64,11... | collective-permute-start | bytes 245768 | tf_op jit(solution)/shard_map/ppermute | solution.py:402
  73.1 21.6 %copy-start.7 = (f32[1024]{0:T(1024)S(1)}, f32[1024]{0:T(1024)}, u32[]{:S(2)}) copy-start(f32[1024]{0:T(1024)} %param.16) | copy-start | bytes 12292
  73.1 4.5 %collective-permute-start.9 = (bf16[80,512]{1,0:T(8,128)(2,1)S(1)}, bf16[80,512]{1,0:T(8,128)(2,1)S(1)}, u32[]{:S(2)}, u32[]{:S(2)}) collective-permute-start(bf16[80,512]{1,0:T(8,128)(2,1)S(1)} %attend.6), channel_id=1, source_target_pairs={{0,16},{8,24},{16,32},{24,40},{32,48},{40,56},{48,0},{56,8},{64,80... | collective-permute-start | bytes 245768 | tf_op jit(solution)/shard_map/ppermute | solution.py:402
  73.8 20.9 %collective-permute-start.11 = (bf16[8,64,1024]{2,1,0:T(8,128)(2,1)S(1)}, bf16[8,64,1024]{2,1,0:T(8,128)(2,1)S(1)}, u32[]{:S(2)}, u32[]{:S(2)}) collective-permute-start(bf16[8,64,1024]{2,1,0:T(8,128)(2,1)S(1)} %all-to-all-done.2._.w_mine), channel_id=1, source_target_pairs={{0,8},{8,0},{16,24},{24,16},{32,40},{40,32},{48,56},{56,48},{64,72... | collective-permute-start | bytes 3145736 | tf_op jit(solution)/shard_map/ppermute | solution.py:405
  75.4 20.2 %copy-start.4 = (bf16[1024,1024]{1,0:T(8,128)(2,1)S(1)}, bf16[1024,1024]{1,0:T(8,128)(2,1)}, u32[]{:S(2)}) copy-start(bf16[1024,1024]{1,0:T(8,128)(2,1)} %weight.1) | copy-start | bytes 6291460
  75.4 20.2 %copy-start.5 = (f32[8,1024]{1,0:T(8,128)S(1)}, f32[8,1024]{1,0:T(8,128)}, u32[]{:S(2)}) copy-start(f32[8,1024]{1,0:T(8,128)} %scale.1) | copy-start | bytes 98308
  75.4 20.2 %copy-start.6 = (f32[8,1024]{1,0:T(8,128)S(1)}, f32[8,1024]{1,0:T(8,128)}, u32[]{:S(2)}) copy-start(f32[8,1024]{1,0:T(8,128)} %shift.1) | copy-start | bytes 98308
  77.7 1.3 %collective-permute-start.10 = (bf16[64,256]{1,0:T(8,128)(2,1)S(1)}, bf16[64,256]{1,0:T(8,128)(2,1)S(1)}, u32[]{:S(2)}, u32[]{:S(2)}) collective-permute-start(bf16[64,256]{1,0:T(8,128)(2,1)S(1)} %get-tuple-element.17), channel_id=1, source_target_pairs={{0,8},{8,0},{16,24},{24,16},{32,40},{40,32},{48,56},{56,48},{64,72... | collective-permute-start | bytes 98312 | tf_op jit(solution)/shard_map/ppermute | solution.py:406

commit v2 on v1

--- a/solution.py
+++ b/solution.py
@@ -111,7 +111,7 @@
     )(parts, pos)
 
 
-def project_kernel(resid, gain, weight, w_out, mine, other, copies, sems):
+def project_kernel(resid, gain, weight, w_out, kv, qt, copies, sems):
     share = w_out.shape[0] // CORES
     start = pl.multiple_of(lax.axis_index("space") % CORES * share, share)
     source = w_out.at[pl.ds(start, share), :]
@@ -125,63 +125,43 @@
     q, k, v = (jnp.dot(x, weight[i], preferred_element_type=F32) for i in range(3))
     low = lax.broadcasted_iota(jnp.int32, (half, 2 * HEAD_DIM), 1) < HEAD_DIM
     upper, lower = k[:half], k[half:]
-    keys = (
-        jnp.where(low, upper, pltpu.roll(lower, HEAD_DIM, 1)),
-        jnp.where(low, pltpu.roll(upper, HEAD_DIM, 1), lower),
-    )
-    turned = [(q * (1.0 / math.sqrt(HEAD_DIM))).T, v.T]
-    queries, values = ((t[:HEAD_DIM], t[HEAD_DIM:]) for t in turned)
-    is_first = lax.axis_index("space") % CORES == 0
-    for ref, (a, b) in ((mine, (0, 1)), (other, (1, 0))):
-        key, value, query = (
-            jnp.where(is_first, pair[a], pair[b]).astype(BF16) for pair in (keys, values, queries)
-        )
-        ref[:half, :] = key
-        for i, turn in ((1, value), (2, query)):
-            ref[i * half : i * half + HEAD_DIM, :] = turn[:, :half]
-            ref[i * half + HEAD_DIM : (i + 1) * half, :] = turn[:, half:]
+    kv[:half, :] = jnp.where(low, upper, pltpu.roll(lower, HEAD_DIM, 1)).astype(BF16)
+    kv[2 * half : 3 * half, :] = jnp.where(low, pltpu.roll(upper, HEAD_DIM, 1), lower).astype(BF16)
+    queries = (q * (1.0 / math.sqrt(HEAD_DIM))).T.astype(BF16)
+    values = v.T.astype(BF16)
+    for head in range(2):
+        for side in range(2):
+            piece = slice(head * HEAD_DIM, (head + 1) * HEAD_DIM), slice(side * half, (side + 1) * half)
+            at = (2 * head + 1) * half + side * HEAD_DIM
+            kv[at : at + HEAD_DIM, :] = values[piece]
+            at = head * half + side * HEAD_DIM
+            qt[at : at + HEAD_DIM, :] = queries[piece]
     for copy in moved:
         copy.wait()
 
 
 def project(resid, gain, weight, w_out, peers):
-    out = shape((resid.shape[0] + 2 * HEAD_DIM, 128), BF16)
+    rows = resid.shape[0]
     return pl.pallas_call(
         project_kernel,
         in_specs=[VMEM] * 4,
         out_specs=(VMEM, VMEM, ANY),
-        out_shape=(out, out, shape((peers, w_out.shape[0] // CORES, D), BF16)),
+        out_shape=(
+            shape((2 * rows, 128), BF16),
+            shape((rows, 128), BF16),
+            shape((peers, w_out.shape[0] // CORES, D), BF16),
+        ),
         scratch_shapes=[pltpu.SemaphoreType.DMA((peers,))],
         compiler_params=PARAMS,
-        cost_estimate=cost(200 << 20, 4<< 20),
+        cost_estimate=cost(200 << 20, 4 << 20),
         name="project",
     )(resid, gain, weight, w_out)
 
 
-def pair_kernel(mine, swapped, kv, qt):
-    rows, turned = kv.shape[0] // 2, qt.shape[0] // 2
-    kv[:rows, :] = mine[:rows, :]
-    kv[rows:, :] = swapped[:rows, :]
-    qt[:turned, :] = mine[rows:, :]
-    qt[turned:, :] = swapped[rows:, :]
-
-
-def pair(mine, swapped):
-    rows = mine.shape[0] - 2 * HEAD_DIM
-    return pl.pallas_call(
-        pair_kernel,
-        in_specs=[VMEM, VMEM],
-        out_specs=(VMEM, VMEM),
-        out_shape=(shape((2 * rows, 128), BF16), shape((4 * HEAD_DIM, 128), BF16)),
-        compiler_params=PARAMS,
-        cost_estimate=cost(1<< 20, 1<< 20),
-        name="pair",
-    )(mine, swapped)
-
-
-def attend_kernel(k0, k1, k2, k3, queries, out):
+def attend_kernel(*args):
+    *pieces, queries, out = args
     zeros = jnp.zeros((HEAD_DIM, 256), BF16)
-    groups = ((k0, k1), (k2, k3))
+    groups = (pieces[:4], pieces[4:])
 
     def scores_of(tile, refs):
         at = tile * 2 * HEAD_DIM
@@ -190,22 +170,21 @@
         )
         sides = jnp.concatenate([turned, zeros], 0), jnp.concatenate([zeros, turned], 0)
         return [
-            jnp.dot(ref[at : at + 128, :], side, preferred_element_type=F32)
+            jnp.dot(ref[tile * 256 : tile * 256 + 128, :], side, preferred_element_type=F32)
             for ref in refs
-            for at in (0, 256)
             for side in sides
         ]
 
-    def merged(state, scores, refs):
+    def merged(state, scores, tile, refs):
         top = functools.reduce(jnp.maximum, [jnp.max(s, 0, keepdims=True) for s in scores]) * LOG2E
         if state is not None:
             top = jnp.maximum(state[0], top)
         probs = [jnp.exp2(s * LOG2E - top) for s in scores]
         total = functools.reduce(jnp.add, [jnp.sum(p, 0, keepdims=True) for p in probs])
         values = [
-            jnp.concatenate([ref[at + 128 : at + 192, :], ref[at + 192 : at + 256, :]], 1)
+            jnp.concatenate([ref[at : at + HEAD_DIM, :], ref[at + HEAD_DIM : at + 2 * HEAD_DIM, :]], 1)
             for ref in refs
-            for at in (0, 256)
+            for at in (tile * 256 + 128,)
         ]
         acc = jnp.zeros((HEAD_DIM, 256), F32)
         for i, value in enumerate(values):
@@ -224,7 +203,7 @@
         scores = ahead
         if i + 1 < len(work):
             ahead = scores_of(*work[i + 1])
-        states[tile] = merged(states[tile], scores, refs)
+        states[tile] = merged(states[tile], scores, tile, refs)
     for tile, (top, total, acc) in enumerate(states):
         lanes = slice(tile * 256, tile * 256 + 256)
         out[:HEAD_DIM, lanes] = (acc / total).astype(BF16)
@@ -238,7 +217,7 @@
     each = key_pieces[0].shape[0]
     return pl.pallas_call(
         attend_kernel,
-        in_specs=[VMEM] * 5,
+        in_specs=[VMEM] * 9,
         out_specs=VMEM,
         out_shape=shape((HEAD_DIM + 16, each), BF16),
         compiler_params=PARAMS,
@@ -247,7 +226,7 @@
     )(*key_pieces, queries)
 
 
-def merge_heads_kernel(p0, p1, p2, p3, mine, other):
+def merge_heads_kernel(p0, p1, p2, p3, out):
     refs = (p0, p1, p2, p3)
     logs = [jnp.sum(r[HEAD_DIM:, :].astype(F32), 0, keepdims=True) for r in refs]
     top = functools.reduce(jnp.maximum, logs)
@@ -257,41 +236,40 @@
     for r, w in zip(refs, weights):
         acc = acc + (w / total) * r[:HEAD_DIM, :].astype(F32)
     half = p0.shape[1] // 2
-    mine[...] = acc[:, :half].astype(BF16)
-    other[...] = acc[:, half:].astype(BF16)
+    is_first = lax.axis_index("space") % CORES == 0
+    a, b = acc[:, :half], acc[:, half:]
+    out[:HEAD_DIM, :] = jnp.where(is_first, a, b)
+    out[HEAD_DIM:, :] = jnp.where(is_first, b, a)
 
 
 def merge_heads(parts):
-    width = parts[0].shape[1] // 2
-    out = shape((HEAD_DIM, width), BF16)
     return pl.pallas_call(
         merge_heads_kernel,
         in_specs=[VMEM] * 4,
-        out_specs=(VMEM, VMEM),
-        out_shape=(out, out),
-        compiler_params=PARAMS,
-        cost_estimate=cost(1<< 20, 1<< 20),
+        out_specs=VMEM,
+        out_shape=shape((2 * HEAD_DIM, parts[0].shape[1] // 2), F32),
+        compiler_params=PARAMS,
+        cost_estimate=cost(1 << 20, 1 << 20),
         name="merge_heads",
     )(*parts)
 
 
-def spread_kernel(mine, other, _, out):
-    both = jnp.concatenate([mine[...].astype(F32), other[...].astype(F32)], 0)
-    value = both.T.astype(BF16)
+def spread_kernel(both, _, out):
+    value = both[...].T.astype(BF16)
     for i in range(out.shape[0]):
         out[i] = value
 
 
-def spread(mine, other, after, peers):
+def spread(both, after, peers):
     return pl.pallas_call(
         spread_kernel,
-        in_specs=[VMEM, VMEM, ANY],
+        in_specs=[VMEM, ANY],
         out_specs=VMEM,
-        out_shape=shape((peers, mine.shape[1], 2 * HEAD_DIM), BF16),
-        compiler_params=PARAMS,
-        cost_estimate=cost(1<< 20, 1<< 20),
+        out_shape=shape((peers, both.shape[1], both.shape[0]), BF16),
+        compiler_params=PARAMS,
+        cost_estimate=cost(1 << 20, 1 << 20),
         name="spread",
-    )(mine, other, after)
+    )(both, after)
 
 
 def trunk_kernel(mixed, w_mine, w_other, resid, gain, normed):
@@ -389,21 +367,22 @@
     parts = exchange(pool(patches, var_embed, agg_query.reshape(1, D), peers))
     resid = exchange(merge_pool(parts, pos_embed)).reshape(rows, D)
 
-    mine, other, copies = project(
+    kv, qt, copies = project(
         resid, gain_first.reshape(1, D), w_qkv.transpose(1, 0, 2), w_out, peers
     )
-    kv, qt = pair(mine, lax.ppermute(other, "space", SWAP))
-    key_pieces = [kv] + [lax.ppermute(kv, "space", along_z(k)) for k in (2, 1, 3)]
+    key_pieces = [lax.ppermute(kv, "space", along_z(k)) for k in (2, 1, 3)]
     query_pieces = [lax.ppermute(qt, "space", along_x(k)) for k in (2, 1, 3)]
     w_mine = exchange(copies)
+    key_pieces = [kv] + key_pieces
+    key_pieces = key_pieces + [lax.ppermute(k, "space", SWAP) for k in key_pieces]
     back = []
     for k, piece in zip((2, 1, 3), query_pieces):
         partial = attend(key_pieces, piece)
         back.append(lax.ppermute(partial, "space", along_x(-k)))
     back.append(attend(key_pieces, qt))
-    mine, other = merge_heads(back)
+    both = merge_heads(back)
+    mixed = exchange(spread(both, w_mine, peers))
     w_other = lax.ppermute(w_mine, "space", SWAP)
-    mixed = exchange(spread(mine, lax.ppermute(other, "space", SWAP), w_mine, peers))
     normed = trunk(mixed, w_mine, w_other, resid, gain_second.reshape(1, D))
     return decode(normed, mod_scale, mod_shift, w_dec)
 

time: 103 us -> 110 us (1.068)
  waiting for transfers between devices: 14.9 us -> 22.7 us
    ppermute x5 -> x7, waiting for transfers between devices: 10.5 us -> 16.2 us  [the longest x3 16.2 us: body(): key_pieces = [lax.ppermute(kv, 'space', along_z(k)) for k in (2, 1, 3)]]
    ppermute x3, waiting for transfers between devices: 2.22 us -> 3.89 us  [body(): query_pieces = [lax.ppermute(qt, 'space', along_x(k)) for k in (2, 1, 3)]]
    ppermute x3, starting transfers between devices: 4.58 us -> 5.79 us  [body(): back.append(lax.ppermute(partial, 'space', along_x(-k)))]
    ppermute x5 -> x7, starting transfers between devices: 9.48 us -> 9.81 us  [the longest x3 9.29 us: body(): key_pieces = [lax.ppermute(kv, 'space', along_z(k)) for k in (2, 1, 3)]]
    pallas_call x7 -> x6, Pallas kernels: 6.53 us -> 6.63 us  [the longest x4 6.42 us: attend(): pl.pallas_call(attend_kernel, in_specs=[VMEM] * 9, out_specs=VMEM, out_sh...]
  transfers between devices with their start and end apart: 13 -> 15, of which waited for: 6 -> 4; matrix products, arithmetic and copies ran while one was open for 0% -> 0% of each run, Pallas kernels for 6% -> 6%
where the time goes in v2:
time: 110 us; the launch traced here: 109 us
  blocking collectives  43.3 us (39%)
  starting transfers between devices  23.3 us (21%)
  waiting for transfers between devices  22.7 us (21%)
  Pallas kernels  19.6 us (18%)
    all_to_all x3, blocking collectives, exchange(): return lax.all_to_all(array, 'chan', 0, 0, tiled=True)  43.3 us
    ppermute x3, waiting for transfers between devices, body(): key_pieces = [lax.ppermute(kv, 'space', along_z(k)) for k in (2, 1, 3)]  16.2 us
    ppermute x3, starting transfers between devices, body(): key_pieces = [lax.ppermute(kv, 'space', along_z(k)) for k in (2, 1, 3)]  9.29 us
    pallas_call x4, Pallas kernels, attend(): pl.pallas_call(attend_kernel, in_specs=[VMEM] * 9, out_specs=VMEM, out_sh...  6.42 us
    pallas_call x1, Pallas kernels, decode(): pl.pallas_call(decode_kernel, grid=(count // each,), in_specs=[VMEM] * 4,...  6.09 us
    ppermute x3, starting transfers between devices, body(): back.append(lax.ppermute(partial, 'space', along_x(-k)))  5.79 us
    pallas_call x1, Pallas kernels, pool(): pl.pallas_call(pool_kernel, grid=(peers // each,), in_specs=[pl.BlockSpec...  4.66 us
    ppermute x3, starting transfers between devices, body(): query_pieces = [lax.ppermute(qt, 'space', along_x(k)) for k in (2, 1, 3)]  4.15 us
  transfers between devices with their start and end apart: 15, of which 4 were waited for; matrix products, arithmetic and copies ran while one was open for 0% of the time, Pallas kernels for 6%

profile of v2, /device:TPU:2, one launch (start us, length us, event | category | flops | bytes accessed | tf_op | source)
XLA Modules:
  0.0 109.2 jit_solution(15668034649499093239)
XLA Ops:
  0.0 0.0 copy-start.1
  0.0 0.0 copy-start
  0.0 0.0 copy-start.2
  0.0 0.0 copy-start.3
  0.0 4.7 %pool.1 = bf16[8,32,1152]{2,1,0:T(8,128)(2,1)} custom-call(bf16[8,256,1024]{2,1,0:T(8,128)(2,1)} %patches.1, f32[8,1024]{1,0:T(8,128)} %var_embed.1, f32[1,1024]{1,0:T(1,128)} %bitcast.10), custom_call_target="tpu_custom_call" | custom-call | flops 16777216 | bytes 8388608 | tf_op jit(solution)/shard_map/pool/pallas_call | solution.py:71
  4.7 16.7 %all_to_all.20.parts = bf16[8,32,1152]{2,1,0:T(8,128)(2,1)S(1)} all-to-all(bf16[8,32,1152]{2,1,0:T(8,128)(2,1)} %pool.1), channel_id=1, replica_groups=mesh['space'=32,'chan'=8] {'chan'}, dimensions={0} | all-to-all | bytes 1179648 | tf_op jit(solution)/shard_map/all_to_all | solution.py:348
  21.4 0.0 copy-done.1
  21.4 0.3 merge_pool.1
  21.7 11.6 %all_to_all.21 = bf16[8,32,1024]{2,1,0:T(8,128)(2,1)S(1)} all-to-all(bf16[8,32,1024]{2,1,0:T(8,128)(2,1)S(1)} %merge_pool.1), channel_id=1, replica_groups=mesh['space'=32,'chan'=8] {'chan'}, dimensions={0} | all-to-all | bytes 1048576 | tf_op jit(solution)/shard_map/all_to_all | solution.py:348
  33.3 0.0 copy-done
  33.3 0.0 copy-done.2
  33.3 0.0 copy-done.3
  33.3 1.1 %project.1 = (bf16[512,128]{1,0:T(8,128)(2,1)S(1)}, bf16[256,128]{1,0:T(8,128)(2,1)S(1)}, bf16[8,64,1024]{2,1,0:T(8,128)(2,1)}) custom-call(bf16[256,1024]{1,0:T(8,128)(2,1)S(1)} %bitcast.5, f32[1,1024]{1,0:T(1,128)S(1)} %bitcast.8, bf16[3,1024,128]{2,1,0:T(8,128)(2,1)S(1)} %bitcast.7, bf16[128,1024]{1,0:T(8,128)(2,1)S(1)} %copy-done.2), custom_call_target="tpu_custom_call" | custom-call | flops 209715200 | bytes 4194304 | tf_op jit(solution)/shard_map/project/pallas_call | solution.py:145
  34.5 3.6 %all-to-all-start.2 = ((bf16[8,64,1024]{2,1,0:T(8,128)(2,1)}), bf16[8,64,1024]{2,1,0:T(8,128)(2,1)S(1)}, u32[]{:S(2)}, u32[]{:S(2)}) async-start(bf16[8,64,1024]{2,1,0:T(8,128)(2,1)} %get-tuple-element.10), calls=%async_computation.2 | async-start | bytes 2097152 | tf_op jit(solution)/shard_map/all_to_all | solution.py:348
  38.0 5.5 %collective-permute-start.2 = (bf16[512,128]{1,0:T(8,128)(2,1)S(1)}, bf16[512,128]{1,0:T(8,128)(2,1)S(1)}, u32[]{:S(2)}, u32[]{:S(2)}) collective-permute-start(bf16[512,128]{1,0:T(8,128)(2,1)S(1)} %get-tuple-element.8.args_0_), channel_id=1, source_target_pairs={{0,192},{8,200},{16,208},{24,216},{32,224},{40,232},{48,240},{56,2... | collective-permute-start | bytes 393224 | tf_op jit(solution)/shard_map/ppermute | solution.py:373
  43.5 0.0 collective-permute-start.1
  43.5 3.8 %collective-permute-start = (bf16[512,128]{1,0:T(8,128)(2,1)S(1)}, bf16[512,128]{1,0:T(8,128)(2,1)S(1)}, u32[]{:S(2)}, u32[]{:S(2)}) collective-permute-start(bf16[512,128]{1,0:T(8,128)(2,1)S(1)} %get-tuple-element.8.args_0_), channel_id=1, source_target_pairs={{0,128},{8,136},{16,144},{24,152},{32,160},{40,168},{48,176},{56,1... | collective-permute-start | bytes 393224 | tf_op jit(solution)/shard_map/ppermute | solution.py:373
  47.3 0.0 collective-permute-start.3
  47.3 0.0 collective-permute-done.2.args_3_
  47.3 0.5 collective-permute-start.6
  47.9 13.8 %collective-permute-done.1.args_2_ = bf16[512,128]{1,0:T(8,128)(2,1)S(1)} collective-permute-done((bf16[512,128]{1,0:T(8,128)(2,1)S(1)}, bf16[512,128]{1,0:T(8,128)(2,1)S(1)}, u32[]{:S(2)}, u32[]{:S(2)}) %collective-permute-start.1) | collective-permute-done | bytes 131104 | tf_op jit(solution)/shard_map/ppermute | solution.py:373
  61.6 0.0 collective-permute-start.5
  61.6 2.4 %collective-permute-done.args_1_ = bf16[512,128]{1,0:T(8,128)(2,1)S(1)} collective-permute-done((bf16[512,128]{1,0:T(8,128)(2,1)S(1)}, bf16[512,128]{1,0:T(8,128)(2,1)S(1)}, u32[]{:S(2)}, u32[]{:S(2)}) %collective-permute-start) | collective-permute-done | bytes 131104 | tf_op jit(solution)/shard_map/ppermute | solution.py:373
  64.0 0.0 collective-permute-start.4
  64.0 2.1 %collective-permute-start.7 = (bf16[256,128]{1,0:T(8,128)(2,1)S(1)}, bf16[256,128]{1,0:T(8,128)(2,1)S(1)}, u32[]{:S(2)}, u32[]{:S(2)}) collective-permute-start(bf16[256,128]{1,0:T(8,128)(2,1)S(1)} %get-tuple-element.9.args_8_), channel_id=1, source_target_pairs={{0,32},{8,40},{16,48},{24,56},{32,0},{40,8},{48,16},{56,24},{64,96... | collective-permute-start | bytes 196616 | tf_op jit(solution)/shard_map/ppermute | solution.py:374
  66.1 3.9 %collective-permute-done.7.args_8_ = bf16[256,128]{1,0:T(8,128)(2,1)S(1)} collective-permute-done((bf16[256,128]{1,0:T(8,128)(2,1)S(1)}, bf16[256,128]{1,0:T(8,128)(2,1)S(1)}, u32[]{:S(2)}, u32[]{:S(2)}) %collective-permute-start.7) | collective-permute-done | bytes 65568 | tf_op jit(solution)/shard_map/ppermute | solution.py:374
  70.0 0.5 collective-permute-start.11
  70.6 0.0 collective-permute-done.3.args_4_
  70.6 1.5 %collective-permute-start.9 = (bf16[256,128]{1,0:T(8,128)(2,1)S(1)}, bf16[256,128]{1,0:T(8,128)(2,1)S(1)}, u32[]{:S(2)}, u32[]{:S(2)}) collective-permute-start(bf16[256,128]{1,0:T(8,128)(2,1)S(1)} %get-tuple-element.9.args_8_), channel_id=1, source_target_pairs={{0,16},{8,24},{16,32},{24,40},{32,48},{40,56},{48,0},{56,8},{64,80... | collective-permute-start | bytes 196616 | tf_op jit(solution)/shard_map/ppermute | solution.py:374
  72.0 0.0 collective-permute-done.6.args_7_
  72.1 0.0 collective-permute-done.5.args_6_
  72.1 0.0 collective-permute-done.4.args_5_
  72.1 1.6 %attend.4 = bf16[80,512]{1,0:T(8,128)(2,1)S(1)} custom-call(bf16[512,128]{1,0:T(8,128)(2,1)S(1)} %get-tuple-element.8.args_0_, bf16[512,128]{1,0:T(8,128)(2,1)S(1)} %collective-permute-done.args_1_, bf16[512,128]{1,0:T(8,128)(2,1)S(1)} %collective-permute-done.1.args_2_, bf16[512,128]{1,0:T(8,128)(2,1)S(1)} %collective-permute-done.2.args_3_, ...), custom_call_target="tpu_custom_call" | custom-call | flops 1073741824 | bytes 2097152 | tf_op jit(solution)/shard_map/attend/pallas_call | solution.py:218
  73.7 3.6 %collective-permute-start.8 = (bf16[80,512]{1,0:T(8,128)(2,1)S(1)}, bf16[80,512]{1,0:T(8,128)(2,1)S(1)}, u32[]{:S(2)}, u32[]{:S(2)}) collective-permute-start(bf16[80,512]{1,0:T(8,128)(2,1)S(1)} %attend.4), channel_id=1, source_target_pairs={{0,32},{8,40},{16,48},{24,56},{32,0},{40,8},{48,16},{56,24},{64,96... | collective-permute-start | bytes 245768 | tf_op jit(solution)/shard_map/ppermute | solution.py:381
  77.3 0.0 collective-permute-done.9.args_8_
  77.3 1.6 %attend.5 = bf16[80,512]{1,0:T(8,128)(2,1)S(1)} custom-call(bf16[512,128]{1,0:T(8,128)(2,1)S(1)} %get-tuple-element.8.args_0_, bf16[512,128]{1,0:T(8,128)(2,1)S(1)} %collective-permute-done.args_1_, bf16[512,128]{1,0:T(8,128)(2,1)S(1)} %collective-permute-done.1.args_2_, bf16[512,128]{1,0:T(8,128)(2,1)S(1)} %collective-permute-done.2.args_3_, ...), custom_call_target="tpu_custom_call" | custom-call | flops 1073741824 | bytes 2097152 | tf_op jit(solution)/shard_map/attend/pallas_call | solution.py:218
  78.9 1.6 %collective-permute-start.10 = (bf16[80,512]{1,0:T(8,128)(2,1)S(1)}, bf16[80,512]{1,0:T(8,128)(2,1)S(1)}, u32[]{:S(2)}, u32[]{:S(2)}) collective-permute-start(bf16[80,512]{1,0:T(8,128)(2,1)S(1)} %attend.5), channel_id=1, source_target_pairs={{0,48},{8,56},{16,0},{24,8},{32,16},{40,24},{48,32},{56,40},{64,11... | collective-permute-start | bytes 245768 | tf_op jit(solution)/shard_map/ppermute | solution.py:381
  80.5 0.0 all-to-all-done.2._.w_mine
  80.5 0.0 collective-permute-start.13
  80.5 0.0 collective-permute-done.11.args_8_
  80.5 1.6 %attend.6 = bf16[80,512]{1,0:T(8,128)(2,1)S(1)} custom-call(bf16[512,128]{1,0:T(8,128)(2,1)S(1)} %get-tuple-element.8.args_0_, bf16[512,128]{1,0:T(8,128)(2,1)S(1)} %collective-permute-done.args_1_, bf16[512,128]{1,0:T(8,128)(2,1)S(1)} %collective-permute-done.1.args_2_, bf16[512,128]{1,0:T(8,128)(2,1)S(1)} %collective-permute-done.2.args_3_, ...), custom_call_target="tpu_custom_call" | custom-call | flops 1073741824 | bytes 2097152 | tf_op jit(solution)/shard_map/attend/pallas_call | solution.py:218
  82.1 0.0 copy-start.7
  82.1 0.6 collective-permute-start.12
  82.7 1.6 %attend.7.p3 = bf16[80,512]{1,0:T(8,128)(2,1)S(1)} custom-call(bf16[512,128]{1,0:T(8,128)(2,1)S(1)} %get-tuple-element.8.args_0_, bf16[512,128]{1,0:T(8,128)(2,1)S(1)} %collective-permute-done.args_1_, bf16[512,128]{1,0:T(8,128)(2,1)S(1)} %collective-permute-done.1.args_2_, bf16[512,128]{1,0:T(8,128)(2,1)S(1)} %collective-permute-done.2.args_3_, ...), custom_call_target="tpu_custom_call" | custom-call | flops 1073741824 | bytes 2097152 | tf_op jit(solution)/shard_map/attend/pallas_call | solution.py:218
  84.3 0.0 copy-start.4
  84.3 0.0 copy-start.5
  84.3 0.0 copy-start.6
  84.4 0.0 collective-permute-done.8.p0
  84.4 0.0 collective-permute-done.10.p1
  84.4 2.7 %collective-permute-done.12.p2 = bf16[80,512]{1,0:T(8,128)(2,1)S(1)} collective-permute-done((bf16[80,512]{1,0:T(8,128)(2,1)S(1)}, bf16[80,512]{1,0:T(8,128)(2,1)S(1)}, u32[]{:S(2)}, u32[]{:S(2)}) %collective-permute-start.12) | collective-permute-done | bytes 81952 | tf_op jit(solution)/shard_map/ppermute | solution.py:381
  87.1 0.1 merge_heads.1.both
  87.2 0.1 spread.1
  87.3 15.0 %all_to_all.22.mixed = bf16[8,256,128]{2,1,0:T(8,128)(2,1)S(1)} all-to-all(bf16[8,256,128]{2,1,0:T(8,128)(2,1)S(1)} %spread.1), channel_id=1, replica_groups=mesh['space'=32,'chan'=8] {'chan'}, dimensions={0} | all-to-all | bytes 1048576 | tf_op jit(solution)/shard_map/all_to_all | solution.py:348
  102.2 0.0 collective-permute-done.13.w_other
  102.2 0.0 copy-done.7
  102.2 0.8 trunk.1.normed
  103.1 0.0 copy-done.4
  103.1 0.0 copy-done.5
  103.1 0.0 copy-done.6
  103.1 6.1 %decode.1 = bf16[8,256,1024]{2,1,0:T(8,128)(2,1)} custom-call(bf16[256,1024]{1,0:T(8,128)(2,1)S(1)} %trunk.1.normed, f32[8,1024]{1,0:T(8,128)S(1)} %copy-done.5, f32[8,1024]{1,0:T(8,128)S(1)} %copy-done.6, bf16[1024,1024]{1,0:T(8,128)(2,1)S(1)} %copy-done.4), custom_call_target="tpu_custom_call" | custom-call | flops 5368709120 | bytes 8388608 | tf_op jit(solution)/shard_map/decode/pallas_call | solution.py:311
Async XLA Ops:
  0.0 21.4 %copy-start.1 = (bf16[256,1024]{1,0:T(8,128)(2,1)S(1)}, bf16[256,1024]{1,0:T(8,128)(2,1)}, u32[]{:S(2)}) copy-start(bf16[256,1024]{1,0:T(8,128)(2,1)} %pos.1) | copy-start | bytes 1572868
  0.0 33.3 %copy-start = (bf16[1024,3,128]{2,0,1:T(8,128)(2,1)S(1)}, bf16[1024,3,128]{2,0,1:T(8,128)(2,1)}, u32[]{:S(2)}) copy-start(bf16[1024,3,128]{2,0,1:T(8,128)(2,1)} %param.17) | copy-start | bytes 2359300
  0.0 33.3 %copy-start.2 = (bf16[128,1024]{1,0:T(8,128)(2,1)S(1)}, bf16[128,1024]{1,0:T(8,128)(2,1)}, u32[]{:S(2)}) copy-start(bf16[128,1024]{1,0:T(8,128)(2,1)} %w_out.1) | copy-start | bytes 786436
  0.0 33.3 %copy-start.3 = (f32[1024]{0:T(1024)S(1)}, f32[1024]{0:T(1024)}, u32[]{:S(2)}) copy-start(f32[1024]{0:T(1024)} %param.15) | copy-start | bytes 12292
  34.5 46.0 %all-to-all-start.2 = ((bf16[8,64,1024]{2,1,0:T(8,128)(2,1)}), bf16[8,64,1024]{2,1,0:T(8,128)(2,1)S(1)}, u32[]{:S(2)}, u32[]{:S(2)}) async-start(bf16[8,64,1024]{2,1,0:T(8,128)(2,1)} %get-tuple-element.10), calls=%async_computation.2 | async-start | bytes 2097152 | tf_op jit(solution)/shard_map/all_to_all | solution.py:348
  38.0 9.3 %collective-permute-start.2 = (bf16[512,128]{1,0:T(8,128)(2,1)S(1)}, bf16[512,128]{1,0:T(8,128)(2,1)S(1)}, u32[]{:S(2)}, u32[]{:S(2)}) collective-permute-start(bf16[512,128]{1,0:T(8,128)(2,1)S(1)} %get-tuple-element.8.args_0_), channel_id=1, source_target_pairs={{0,192},{8,200},{16,208},{24,216},{32,224},{40,232},{48,240},{56,2... | collective-permute-start | bytes 393224 | tf_op jit(solution)/shard_map/ppermute | solution.py:373
  43.5 18.1 %collective-permute-start.1 = (bf16[512,128]{1,0:T(8,128)(2,1)S(1)}, bf16[512,128]{1,0:T(8,128)(2,1)S(1)}, u32[]{:S(2)}, u32[]{:S(2)}) collective-permute-start(bf16[512,128]{1,0:T(8,128)(2,1)S(1)} %get-tuple-element.8.args_0_), channel_id=1, source_target_pairs={{0,64},{8,72},{16,80},{24,88},{32,96},{40,104},{48,112},{56,120},{... | collective-permute-start | bytes 393224 | tf_op jit(solution)/shard_map/ppermute | solution.py:373
  43.5 20.5 %collective-permute-start = (bf16[512,128]{1,0:T(8,128)(2,1)S(1)}, bf16[512,128]{1,0:T(8,128)(2,1)S(1)}, u32[]{:S(2)}, u32[]{:S(2)}) collective-permute-start(bf16[512,128]{1,0:T(8,128)(2,1)S(1)} %get-tuple-element.8.args_0_), channel_id=1, source_target_pairs={{0,128},{8,136},{16,144},{24,152},{32,160},{40,168},{48,176},{56,1... | collective-permute-start | bytes 393224 | tf_op jit(solution)/shard_map/ppermute | solution.py:373
  47.3 23.2 %collective-permute-start.3 = (bf16[512,128]{1,0:T(8,128)(2,1)S(1)}, bf16[512,128]{1,0:T(8,128)(2,1)S(1)}, u32[]{:S(2)}, u32[]{:S(2)}) collective-permute-start(bf16[512,128]{1,0:T(8,128)(2,1)S(1)} %get-tuple-element.8.args_0_), channel_id=1, source_target_pairs={{0,8},{8,0},{16,24},{24,16},{32,40},{40,32},{48,56},{56,48},{64,72... | collective-permute-start | bytes 393224 | tf_op jit(solution)/shard_map/ppermute | solution.py:377
  47.3 24.7 %collective-permute-start.6 = (bf16[512,128]{1,0:T(8,128)(2,1)S(1)}, bf16[512,128]{1,0:T(8,128)(2,1)S(1)}, u32[]{:S(2)}, u32[]{:S(2)}) collective-permute-start(bf16[512,128]{1,0:T(8,128)(2,1)S(1)} %collective-permute-done.2.args_3_), channel_id=1, source_target_pairs={{0,8},{8,0},{16,24},{24,16},{32,40},{40,32},{48,56},{56,48},{64,72... | collective-permute-start | bytes 393224 | tf_op jit(solution)/shard_map/ppermute | solution.py:377
  61.6 10.4 %collective-permute-start.5 = (bf16[512,128]{1,0:T(8,128)(2,1)S(1)}, bf16[512,128]{1,0:T(8,128)(2,1)S(1)}, u32[]{:S(2)}, u32[]{:S(2)}) collective-permute-start(bf16[512,128]{1,0:T(8,128)(2,1)S(1)} %collective-permute-done.1.args_2_), channel_id=1, source_target_pairs={{0,8},{8,0},{16,24},{24,16},{32,40},{40,32},{48,56},{56,48},{64,72... | collective-permute-start | bytes 393224 | tf_op jit(solution)/shard_map/ppermute | solution.py:377
  64.0 8.1 %collective-permute-start.4 = (bf16[512,128]{1,0:T(8,128)(2,1)S(1)}, bf16[512,128]{1,0:T(8,128)(2,1)S(1)}, u32[]{:S(2)}, u32[]{:S(2)}) collective-permute-start(bf16[512,128]{1,0:T(8,128)(2,1)S(1)} %collective-permute-done.args_1_), channel_id=1, source_target_pairs={{0,8},{8,0},{16,24},{24,16},{32,40},{40,32},{48,56},{56,48},{64,72... | collective-permute-start | bytes 393224 | tf_op jit(solution)/shard_map/ppermute | solution.py:377
  64.0 6.0 %collective-permute-start.7 = (bf16[256,128]{1,0:T(8,128)(2,1)S(1)}, bf16[256,128]{1,0:T(8,128)(2,1)S(1)}, u32[]{:S(2)}, u32[]{:S(2)}) collective-permute-start(bf16[256,128]{1,0:T(8,128)(2,1)S(1)} %get-tuple-element.9.args_8_), channel_id=1, source_target_pairs={{0,32},{8,40},{16,48},{24,56},{32,0},{40,8},{48,16},{56,24},{64,96... | collective-permute-start | bytes 196616 | tf_op jit(solution)/shard_map/ppermute | solution.py:374
  70.0 10.5 %collective-permute-start.11 = (bf16[256,128]{1,0:T(8,128)(2,1)S(1)}, bf16[256,128]{1,0:T(8,128)(2,1)S(1)}, u32[]{:S(2)}, u32[]{:S(2)}) collective-permute-start(bf16[256,128]{1,0:T(8,128)(2,1)S(1)} %get-tuple-element.9.args_8_), channel_id=1, source_target_pairs={{0,48},{8,56},{16,0},{24,8},{32,16},{40,24},{48,32},{56,40},{64,11... | collective-permute-start | bytes 196616 | tf_op jit(solution)/shard_map/ppermute | solution.py:374
  70.6 6.7 %collective-permute-start.9 = (bf16[256,128]{1,0:T(8,128)(2,1)S(1)}, bf16[256,128]{1,0:T(8,128)(2,1)S(1)}, u32[]{:S(2)}, u32[]{:S(2)}) collective-permute-start(bf16[256,128]{1,0:T(8,128)(2,1)S(1)} %get-tuple-element.9.args_8_), channel_id=1, source_target_pairs={{0,16},{8,24},{16,32},{24,40},{32,48},{40,56},{48,0},{56,8},{64,80... | collective-permute-start | bytes 196616 | tf_op jit(solution)/shard_map/ppermute | solution.py:374
  73.7 10.7 %collective-permute-start.8 = (bf16[80,512]{1,0:T(8,128)(2,1)S(1)}, bf16[80,512]{1,0:T(8,128)(2,1)S(1)}, u32[]{:S(2)}, u32[]{:S(2)}) collective-permute-start(bf16[80,512]{1,0:T(8,128)(2,1)S(1)} %attend.4), channel_id=1, source_target_pairs={{0,32},{8,40},{16,48},{24,56},{32,0},{40,8},{48,16},{56,24},{64,96... | collective-permute-start | bytes 245768 | tf_op jit(solution)/shard_map/ppermute | solution.py:381
  78.9 5.5 %collective-permute-start.10 = (bf16[80,512]{1,0:T(8,128)(2,1)S(1)}, bf16[80,512]{1,0:T(8,128)(2,1)S(1)}, u32[]{:S(2)}, u32[]{:S(2)}) collective-permute-start(bf16[80,512]{1,0:T(8,128)(2,1)S(1)} %attend.5), channel_id=1, source_target_pairs={{0,48},{8,56},{16,0},{24,8},{32,16},{40,24},{48,32},{56,40},{64,11... | collective-permute-start | bytes 245768 | tf_op jit(solution)/shard_map/ppermute | solution.py:381
  80.5 21.7 %collective-permute-start.13 = (bf16[8,64,1024]{2,1,0:T(8,128)(2,1)S(1)}, bf16[8,64,1024]{2,1,0:T(8,128)(2,1)S(1)}, u32[]{:S(2)}, u32[]{:S(2)}) collective-permute-start(bf16[8,64,1024]{2,1,0:T(8,128)(2,1)S(1)} %all-to-all-done.2._.w_mine), channel_id=1, source_target_pairs={{0,8},{8,0},{16,24},{24,16},{32,40},{40,32},{48,56},{56,48},{64,72... | collective-permute-start | bytes 3145736 | tf_op jit(solution)/shard_map/ppermute | solution.py:385
  82.1 20.1 %copy-start.7 = (f32[1024]{0:T(1024)S(1)}, f32[1024]{0:T(1024)}, u32[]{:S(2)}) copy-start(f32[1024]{0:T(1024)} %param.16) | copy-start | bytes 12292
  82.1 4.9 %collective-permute-start.12 = (bf16[80,512]{1,0:T(8,128)(2,1)S(1)}, bf16[80,512]{1,0:T(8,128)(2,1)S(1)}, u32[]{:S(2)}, u32[]{:S(2)}) collective-permute-start(bf16[80,512]{1,0:T(8,128)(2,1)S(1)} %attend.6), channel_id=1, source_target_pairs={{0,16},{8,24},{16,32},{24,40},{32,48},{40,56},{48,0},{56,8},{64,80... | collective-permute-start | bytes 245768 | tf_op jit(solution)/shard_map/ppermute | solution.py:381
  84.3 18.8 %copy-start.4 = (bf16[1024,1024]{1,0:T(8,128)(2,1)S(1)}, bf16[1024,1024]{1,0:T(8,128)(2,1)}, u32[]{:S(2)}) copy-start(bf16[1024,1024]{1,0:T(8,128)(2,1)} %weight.1) | copy-start | bytes 6291460
  84.3 18.8 %copy-start.5 = (f32[8,1024]{1,0:T(8,128)S(1)}, f32[8,1024]{1,0:T(8,128)}, u32[]{:S(2)}) copy-start(f32[8,1024]{1,0:T(8,128)} %scale.1) | copy-start | bytes 98308
  84.3 18.8 %copy-start.6 = (f32[8,1024]{1,0:T(8,128)S(1)}, f32[8,1024]{1,0:T(8,128)}, u32[]{:S(2)}) copy-start(f32[8,1024]{1,0:T(8,128)} %shift.1) | copy-start | bytes 98308

commit v3 on v2

--- a/solution.py
+++ b/solution.py
@@ -40,7 +40,9 @@
 
 def pool_kernel(patches, var_embed, query, out):
     count = patches.shape[0]
-    parts, rows, _ = out.shape
+    rows = out.shape[1]
+    parts = patches.shape[1] // rows
+    first = pl.program_id(0) * parts
     scaled = query[...] * (LOG2E / math.sqrt(D))
     shared = jnp.sum(var_embed[...] * scaled, -1, keepdims=True)
     lane = lax.broadcasted_iota(jnp.int32, (rows, 128), 1)
@@ -58,10 +60,10 @@
         for v in range(count):
             embedded = patches[v, here].astype(F32) + var_embed[v : v + 1, :]
             acc = acc + (expo[v] * inverse) * embedded
-        out[part, :, :D] = acc.astype(BF16)
+        out[first + part, :, :D] = acc.astype(BF16)
         high, mid, low = in_three(top + jnp.log2(total))
         packed = jnp.where(lane == 0, high, jnp.where(lane == 1, mid, jnp.where(lane == 2, low, 0.0)))
-        out[part, :, D:] = packed.astype(BF16)
+        out[first + part, :, D:] = packed.astype(BF16)
 
 
 def pool(patches, var_embed, query, peers):
@@ -76,8 +78,9 @@
             pl.BlockSpec((count, D), lambda i: (0, 0)),
             pl.BlockSpec((1, D), lambda i: (0, 0)),
         ],
-        out_specs=pl.BlockSpec((each, part, D + 128), lambda i: (i, 0, 0)),
+        out_specs=VMEM,
         out_shape=shape((peers, part, D + 128), BF16),
+        compiler_params=pltpu.CompilerParams(vmem_limit_bytes=52 << 20),
         cost_estimate=cost(16 << 20, 8 << 20),
         name="pool",
     )(patches, var_embed, query)

time: 110 us -> 110 us (level)
  local copies, waits for them, and re-layouts: 0.04 us -> 1.54 us
    unnamed x16 -> x20, local copies, waits for them, and re-layouts: 0.04 us -> 1.54 us
where the time goes in v3:
time: 110 us
  blocking collectives  43.1 us (39%)
  starting transfers between devices  23.3 us (21%)
  waiting for transfers between devices  22.7 us (21%)
  Pallas kernels  18.9 us (17%)
  local copies, waits for them, and re-layouts  1.54 us (1%)
    all_to_all x3, blocking collectives, exchange(): return lax.all_to_all(array, 'chan', 0, 0, tiled=True)  43.1 us
    ppermute x3, waiting for transfers between devices, body(): key_pieces = [lax.ppermute(kv, 'space', along_z(k)) for k in (2, 1, 3)]  16.2 us
    ppermute x3, starting transfers between devices, body(): key_pieces = [lax.ppermute(kv, 'space', along_z(k)) for k in (2, 1, 3)]  9.29 us
    pallas_call x4, Pallas kernels, attend(): pl.pallas_call(attend_kernel, in_specs=[VMEM] * 9, out_specs=VMEM, out_sh...  6.42 us
    pallas_call x1, Pallas kernels, decode(): pl.pallas_call(decode_kernel, grid=(count // each,), in_specs=[VMEM] * 4,...  6.09 us
    ppermute x3, starting transfers between devices, body(): back.append(lax.ppermute(partial, 'space', along_x(-k)))  5.78 us
    ppermute x3, starting transfers between devices, body(): query_pieces = [lax.ppermute(qt, 'space', along_x(k)) for k in (2, 1, 3)]  4.15 us
    pallas_call x1, Pallas kernels, pool(): pl.pallas_call(pool_kernel, grid=(peers // each,), in_specs=[pl.BlockSpec...  3.91 us
  transfers between devices with their start and end apart: 15, of which 4 were waited for; matrix products, arithmetic and copies ran while one was open for 0% of the time, Pallas kernels for 6%

profile of v3, /device:TPU:2, one launch (start us, length us, event | category | flops | bytes accessed | tf_op | source)
XLA Modules:
  0.0 109.8 jit_solution(18060407973778347907)
XLA Ops:
  0.0 0.0 copy-start.1
  0.0 0.0 copy-start.3
  0.0 0.8 copy-done.3
  0.8 0.0 copy-start.5
  0.8 0.7 copy-done.5
  1.5 0.0 copy-start
  1.5 0.0 copy-start.2
  1.5 0.0 copy-start.4
  1.5 3.9 %pool.1 = bf16[8,32,1152]{2,1,0:T(8,128)(2,1)S(1)} custom-call(bf16[8,256,1024]{2,1,0:T(8,128)(2,1)} %patches.1, f32[8,1024]{1,0:T(8,128)S(1)} %copy-done.3, f32[1,1024]{1,0:T(1,128)S(1)} %bitcast.9), custom_call_target="tpu_custom_call" | custom-call | flops 16777216 | bytes 8388608 | tf_op jit(solution)/shard_map/pool/pallas_call | solution.py:73
  5.4 16.5 %all_to_all.20.parts = bf16[8,32,1152]{2,1,0:T(8,128)(2,1)S(1)} all-to-all(bf16[8,32,1152]{2,1,0:T(8,128)(2,1)S(1)} %pool.1), channel_id=1, replica_groups=mesh['space'=32,'chan'=8] {'chan'}, dimensions={0} | all-to-all | bytes 1179648 | tf_op jit(solution)/shard_map/all_to_all | solution.py:351
  22.0 0.0 copy-done.1
  22.0 0.3 merge_pool.1
  22.2 11.6 %all_to_all.21 = bf16[8,32,1024]{2,1,0:T(8,128)(2,1)S(1)} all-to-all(bf16[8,32,1024]{2,1,0:T(8,128)(2,1)S(1)} %merge_pool.1), channel_id=1, replica_groups=mesh['space'=32,'chan'=8] {'chan'}, dimensions={0} | all-to-all | bytes 1048576 | tf_op jit(solution)/shard_map/all_to_all | solution.py:351
  33.9 0.0 copy-done
  33.9 0.0 copy-done.2
  33.9 0.0 copy-done.4
  33.9 1.1 %project.1 = (bf16[512,128]{1,0:T(8,128)(2,1)S(1)}, bf16[256,128]{1,0:T(8,128)(2,1)S(1)}, bf16[8,64,1024]{2,1,0:T(8,128)(2,1)}) custom-call(bf16[256,1024]{1,0:T(8,128)(2,1)S(1)} %bitcast.5, f32[1,1024]{1,0:T(1,128)S(1)} %bitcast.8, bf16[3,1024,128]{2,1,0:T(8,128)(2,1)S(1)} %bitcast.7, bf16[128,1024]{1,0:T(8,128)(2,1)S(1)} %copy-done.2), custom_call_target="tpu_custom_call" | custom-call | flops 209715200 | bytes 4194304 | tf_op jit(solution)/shard_map/project/pallas_call | solution.py:148
  35.0 3.6 %all-to-all-start.2 = ((bf16[8,64,1024]{2,1,0:T(8,128)(2,1)}), bf16[8,64,1024]{2,1,0:T(8,128)(2,1)S(1)}, u32[]{:S(2)}, u32[]{:S(2)}) async-start(bf16[8,64,1024]{2,1,0:T(8,128)(2,1)} %get-tuple-element.10), calls=%async_computation.2 | async-start | bytes 2097152 | tf_op jit(solution)/shard_map/all_to_all | solution.py:351
  38.6 5.5 %collective-permute-start.2 = (bf16[512,128]{1,0:T(8,128)(2,1)S(1)}, bf16[512,128]{1,0:T(8,128)(2,1)S(1)}, u32[]{:S(2)}, u32[]{:S(2)}) collective-permute-start(bf16[512,128]{1,0:T(8,128)(2,1)S(1)} %get-tuple-element.8.args_0_), channel_id=1, source_target_pairs={{0,192},{8,200},{16,208},{24,216},{32,224},{40,232},{48,240},{56,2... | collective-permute-start | bytes 393224 | tf_op jit(solution)/shard_map/ppermute | solution.py:376
  44.1 0.0 collective-permute-start.1
  44.1 3.8 %collective-permute-start = (bf16[512,128]{1,0:T(8,128)(2,1)S(1)}, bf16[512,128]{1,0:T(8,128)(2,1)S(1)}, u32[]{:S(2)}, u32[]{:S(2)}) collective-permute-start(bf16[512,128]{1,0:T(8,128)(2,1)S(1)} %get-tuple-element.8.args_0_), channel_id=1, source_target_pairs={{0,128},{8,136},{16,144},{24,152},{32,160},{40,168},{48,176},{56,1... | collective-permute-start | bytes 393224 | tf_op jit(solution)/shard_map/ppermute | solution.py:376
  47.9 0.0 collective-permute-start.3
  47.9 0.0 collective-permute-done.2.args_3_
  47.9 0.5 collective-permute-start.6
  48.4 13.8 %collective-permute-done.1.args_2_ = bf16[512,128]{1,0:T(8,128)(2,1)S(1)} collective-permute-done((bf16[512,128]{1,0:T(8,128)(2,1)S(1)}, bf16[512,128]{1,0:T(8,128)(2,1)S(1)}, u32[]{:S(2)}, u32[]{:S(2)}) %collective-permute-start.1) | collective-permute-done | bytes 131104 | tf_op jit(solution)/shard_map/ppermute | solution.py:376
  62.2 0.0 collective-permute-start.5
  62.2 2.4 %collective-permute-done.args_1_ = bf16[512,128]{1,0:T(8,128)(2,1)S(1)} collective-permute-done((bf16[512,128]{1,0:T(8,128)(2,1)S(1)}, bf16[512,128]{1,0:T(8,128)(2,1)S(1)}, u32[]{:S(2)}, u32[]{:S(2)}) %collective-permute-start) | collective-permute-done | bytes 131104 | tf_op jit(solution)/shard_map/ppermute | solution.py:376
  64.6 0.0 collective-permute-start.4
  64.6 2.1 %collective-permute-start.7 = (bf16[256,128]{1,0:T(8,128)(2,1)S(1)}, bf16[256,128]{1,0:T(8,128)(2,1)S(1)}, u32[]{:S(2)}, u32[]{:S(2)}) collective-permute-start(bf16[256,128]{1,0:T(8,128)(2,1)S(1)} %get-tuple-element.9.args_8_), channel_id=1, source_target_pairs={{0,32},{8,40},{16,48},{24,56},{32,0},{40,8},{48,16},{56,24},{64,96... | collective-permute-start | bytes 196616 | tf_op jit(solution)/shard_map/ppermute | solution.py:377
  66.7 3.9 %collective-permute-done.7.args_8_ = bf16[256,128]{1,0:T(8,128)(2,1)S(1)} collective-permute-done((bf16[256,128]{1,0:T(8,128)(2,1)S(1)}, bf16[256,128]{1,0:T(8,128)(2,1)S(1)}, u32[]{:S(2)}, u32[]{:S(2)}) %collective-permute-start.7) | collective-permute-done | bytes 65568 | tf_op jit(solution)/shard_map/ppermute | solution.py:377
  70.6 0.5 collective-permute-start.11
  71.1 0.0 collective-permute-done.3.args_4_
  71.1 1.5 %collective-permute-start.9 = (bf16[256,128]{1,0:T(8,128)(2,1)S(1)}, bf16[256,128]{1,0:T(8,128)(2,1)S(1)}, u32[]{:S(2)}, u32[]{:S(2)}) collective-permute-start(bf16[256,128]{1,0:T(8,128)(2,1)S(1)} %get-tuple-element.9.args_8_), channel_id=1, source_target_pairs={{0,16},{8,24},{16,32},{24,40},{32,48},{40,56},{48,0},{56,8},{64,80... | collective-permute-start | bytes 196616 | tf_op jit(solution)/shard_map/ppermute | solution.py:377
  72.6 0.0 collective-permute-done.6.args_7_
  72.6 0.0 collective-permute-done.5.args_6_
  72.6 0.0 collective-permute-done.4.args_5_
  72.6 1.6 %attend.4 = bf16[80,512]{1,0:T(8,128)(2,1)S(1)} custom-call(bf16[512,128]{1,0:T(8,128)(2,1)S(1)} %get-tuple-element.8.args_0_, bf16[512,128]{1,0:T(8,128)(2,1)S(1)} %collective-permute-done.args_1_, bf16[512,128]{1,0:T(8,128)(2,1)S(1)} %collective-permute-done.1.args_2_, bf16[512,128]{1,0:T(8,128)(2,1)S(1)} %collective-permute-done.2.args_3_, ...), custom_call_target="tpu_custom_call" | custom-call | flops 1073741824 | bytes 2097152 | tf_op jit(solution)/shard_map/attend/pallas_call | solution.py:221
  74.2 3.6 %collective-permute-start.8 = (bf16[80,512]{1,0:T(8,128)(2,1)S(1)}, bf16[80,512]{1,0:T(8,128)(2,1)S(1)}, u32[]{:S(2)}, u32[]{:S(2)}) collective-permute-start(bf16[80,512]{1,0:T(8,128)(2,1)S(1)} %attend.4), channel_id=1, source_target_pairs={{0,32},{8,40},{16,48},{24,56},{32,0},{40,8},{48,16},{56,24},{64,96... | collective-permute-start | bytes 245768 | tf_op jit(solution)/shard_map/ppermute | solution.py:384
  77.8 0.0 collective-permute-done.9.args_8_
  77.8 1.6 %attend.5 = bf16[80,512]{1,0:T(8,128)(2,1)S(1)} custom-call(bf16[512,128]{1,0:T(8,128)(2,1)S(1)} %get-tuple-element.8.args_0_, bf16[512,128]{1,0:T(8,128)(2,1)S(1)} %collective-permute-done.args_1_, bf16[512,128]{1,0:T(8,128)(2,1)S(1)} %collective-permute-done.1.args_2_, bf16[512,128]{1,0:T(8,128)(2,1)S(1)} %collective-permute-done.2.args_3_, ...), custom_call_target="tpu_custom_call" | custom-call | flops 1073741824 | bytes 2097152 | tf_op jit(solution)/shard_map/attend/pallas_call | solution.py:221
  79.4 1.6 %collective-permute-start.10 = (bf16[80,512]{1,0:T(8,128)(2,1)S(1)}, bf16[80,512]{1,0:T(8,128)(2,1)S(1)}, u32[]{:S(2)}, u32[]{:S(2)}) collective-permute-start(bf16[80,512]{1,0:T(8,128)(2,1)S(1)} %attend.5), channel_id=1, source_target_pairs={{0,48},{8,56},{16,0},{24,8},{32,16},{40,24},{48,32},{56,40},{64,11... | collective-permute-start | bytes 245768 | tf_op jit(solution)/shard_map/ppermute | solution.py:384
  81.0 0.0 all-to-all-done.2._.w_mine
  81.0 0.0 collective-permute-start.13
  81.1 0.0 collective-permute-done.11.args_8_
  81.1 1.6 %attend.6 = bf16[80,512]{1,0:T(8,128)(2,1)S(1)} custom-call(bf16[512,128]{1,0:T(8,128)(2,1)S(1)} %get-tuple-element.8.args_0_, bf16[512,128]{1,0:T(8,128)(2,1)S(1)} %collective-permute-done.args_1_, bf16[512,128]{1,0:T(8,128)(2,1)S(1)} %collective-permute-done.1.args_2_, bf16[512,128]{1,0:T(8,128)(2,1)S(1)} %collective-permute-done.2.args_3_, ...), custom_call_target="tpu_custom_call" | custom-call | flops 1073741824 | bytes 2097152 | tf_op jit(solution)/shard_map/attend/pallas_call | solution.py:221
  82.7 0.0 copy-start.9
  82.7 0.6 collective-permute-start.12
  83.3 1.6 %attend.7.p3 = bf16[80,512]{1,0:T(8,128)(2,1)S(1)} custom-call(bf16[512,128]{1,0:T(8,128)(2,1)S(1)} %get-tuple-element.8.args_0_, bf16[512,128]{1,0:T(8,128)(2,1)S(1)} %collective-permute-done.args_1_, bf16[512,128]{1,0:T(8,128)(2,1)S(1)} %collective-permute-done.1.args_2_, bf16[512,128]{1,0:T(8,128)(2,1)S(1)} %collective-permute-done.2.args_3_, ...), custom_call_target="tpu_custom_call" | custom-call | flops 1073741824 | bytes 2097152 | tf_op jit(solution)/shard_map/attend/pallas_call | solution.py:221
  84.9 0.0 copy-start.6
  84.9 0.0 copy-start.7
  84.9 0.0 copy-start.8
  84.9 0.0 collective-permute-done.8.p0
  84.9 0.0 collective-permute-done.10.p1
  84.9 2.7 %collective-permute-done.12.p2 = bf16[80,512]{1,0:T(8,128)(2,1)S(1)} collective-permute-done((bf16[80,512]{1,0:T(8,128)(2,1)S(1)}, bf16[80,512]{1,0:T(8,128)(2,1)S(1)}, u32[]{:S(2)}, u32[]{:S(2)}) %collective-permute-start.12) | collective-permute-done | bytes 81952 | tf_op jit(solution)/shard_map/ppermute | solution.py:384
  87.6 0.1 merge_heads.1.both
  87.7 0.1 spread.1
  87.8 14.9 %all_to_all.22.mixed = bf16[8,256,128]{2,1,0:T(8,128)(2,1)S(1)} all-to-all(bf16[8,256,128]{2,1,0:T(8,128)(2,1)S(1)} %spread.1), channel_id=1, replica_groups=mesh['space'=32,'chan'=8] {'chan'}, dimensions={0} | all-to-all | bytes 1048576 | tf_op jit(solution)/shard_map/all_to_all | solution.py:351
  102.8 0.0 collective-permute-done.13.w_other
  102.8 0.0 copy-done.9
  102.8 0.9 trunk.1.normed
  103.7 0.0 copy-done.6
  103.7 0.0 copy-done.7
  103.7 0.0 copy-done.8
  103.7 6.1 %decode.1 = bf16[8,256,1024]{2,1,0:T(8,128)(2,1)} custom-call(bf16[256,1024]{1,0:T(8,128)(2,1)S(1)} %trunk.1.normed, f32[8,1024]{1,0:T(8,128)S(1)} %copy-done.7, f32[8,1024]{1,0:T(8,128)S(1)} %copy-done.8, bf16[1024,1024]{1,0:T(8,128)(2,1)S(1)} %copy-done.6), custom_call_target="tpu_custom_call" | custom-call | flops 5368709120 | bytes 8388608 | tf_op jit(solution)/shard_map/decode/pallas_call | solution.py:314
Async XLA Ops:
  0.0 22.0 %copy-start.1 = (bf16[256,1024]{1,0:T(8,128)(2,1)S(1)}, bf16[256,1024]{1,0:T(8,128)(2,1)}, u32[]{:S(2)}) copy-start(bf16[256,1024]{1,0:T(8,128)(2,1)} %pos.1) | copy-start | bytes 1572868
  0.0 0.8 copy-start.3
  0.8 0.7 copy-start.5
  1.5 32.4 %copy-start = (bf16[1024,3,128]{2,0,1:T(8,128)(2,1)S(1)}, bf16[1024,3,128]{2,0,1:T(8,128)(2,1)}, u32[]{:S(2)}) copy-start(bf16[1024,3,128]{2,0,1:T(8,128)(2,1)} %param.17) | copy-start | bytes 2359300
  1.5 32.4 %copy-start.2 = (bf16[128,1024]{1,0:T(8,128)(2,1)S(1)}, bf16[128,1024]{1,0:T(8,128)(2,1)}, u32[]{:S(2)}) copy-start(bf16[128,1024]{1,0:T(8,128)(2,1)} %w_out.1) | copy-start | bytes 786436
  1.5 32.4 %copy-start.4 = (f32[1024]{0:T(1024)S(1)}, f32[1024]{0:T(1024)}, u32[]{:S(2)}) copy-start(f32[1024]{0:T(1024)} %param.15) | copy-start | bytes 12292
  35.0 46.0 %all-to-all-start.2 = ((bf16[8,64,1024]{2,1,0:T(8,128)(2,1)}), bf16[8,64,1024]{2,1,0:T(8,128)(2,1)S(1)}, u32[]{:S(2)}, u32[]{:S(2)}) async-start(bf16[8,64,1024]{2,1,0:T(8,128)(2,1)} %get-tuple-element.10), calls=%async_computation.2 | async-start | bytes 2097152 | tf_op jit(solution)/shard_map/all_to_all | solution.py:351
  38.6 9.3 %collective-permute-start.2 = (bf16[512,128]{1,0:T(8,128)(2,1)S(1)}, bf16[512,128]{1,0:T(8,128)(2,1)S(1)}, u32[]{:S(2)}, u32[]{:S(2)}) collective-permute-start(bf16[512,128]{1,0:T(8,128)(2,1)S(1)} %get-tuple-element.8.args_0_), channel_id=1, source_target_pairs={{0,192},{8,200},{16,208},{24,216},{32,224},{40,232},{48,240},{56,2... | collective-permute-start | bytes 393224 | tf_op jit(solution)/shard_map/ppermute | solution.py:376
  44.1 18.1 %collective-permute-start.1 = (bf16[512,128]{1,0:T(8,128)(2,1)S(1)}, bf16[512,128]{1,0:T(8,128)(2,1)S(1)}, u32[]{:S(2)}, u32[]{:S(2)}) collective-permute-start(bf16[512,128]{1,0:T(8,128)(2,1)S(1)} %get-tuple-element.8.args_0_), channel_id=1, source_target_pairs={{0,64},{8,72},{16,80},{24,88},{32,96},{40,104},{48,112},{56,120},{... | collective-permute-start | bytes 393224 | tf_op jit(solution)/shard_map/ppermute | solution.py:376
  44.1 20.5 %collective-permute-start = (bf16[512,128]{1,0:T(8,128)(2,1)S(1)}, bf16[512,128]{1,0:T(8,128)(2,1)S(1)}, u32[]{:S(2)}, u32[]{:S(2)}) collective-permute-start(bf16[512,128]{1,0:T(8,128)(2,1)S(1)} %get-tuple-element.8.args_0_), channel_id=1, source_target_pairs={{0,128},{8,136},{16,144},{24,152},{32,160},{40,168},{48,176},{56,1... | collective-permute-start | bytes 393224 | tf_op jit(solution)/shard_map/ppermute | solution.py:376
  47.9 23.2 %collective-permute-start.3 = (bf16[512,128]{1,0:T(8,128)(2,1)S(1)}, bf16[512,128]{1,0:T(8,128)(2,1)S(1)}, u32[]{:S(2)}, u32[]{:S(2)}) collective-permute-start(bf16[512,128]{1,0:T(8,128)(2,1)S(1)} %get-tuple-element.8.args_0_), channel_id=1, source_target_pairs={{0,8},{8,0},{16,24},{24,16},{32,40},{40,32},{48,56},{56,48},{64,72... | collective-permute-start | bytes 393224 | tf_op jit(solution)/shard_map/ppermute | solution.py:380
  47.9 24.7 %collective-permute-start.6 = (bf16[512,128]{1,0:T(8,128)(2,1)S(1)}, bf16[512,128]{1,0:T(8,128)(2,1)S(1)}, u32[]{:S(2)}, u32[]{:S(2)}) collective-permute-start(bf16[512,128]{1,0:T(8,128)(2,1)S(1)} %collective-permute-done.2.args_3_), channel_id=1, source_target_pairs={{0,8},{8,0},{16,24},{24,16},{32,40},{40,32},{48,56},{56,48},{64,72... | collective-permute-start | bytes 393224 | tf_op jit(solution)/shard_map/ppermute | solution.py:380
  62.2 10.4 %collective-permute-start.5 = (bf16[512,128]{1,0:T(8,128)(2,1)S(1)}, bf16[512,128]{1,0:T(8,128)(2,1)S(1)}, u32[]{:S(2)}, u32[]{:S(2)}) collective-permute-start(bf16[512,128]{1,0:T(8,128)(2,1)S(1)} %collective-permute-done.1.args_2_), channel_id=1, source_target_pairs={{0,8},{8,0},{16,24},{24,16},{32,40},{40,32},{48,56},{56,48},{64,72... | collective-permute-start | bytes 393224 | tf_op jit(solution)/shard_map/ppermute | solution.py:380
  64.6 8.1 %collective-permute-start.4 = (bf16[512,128]{1,0:T(8,128)(2,1)S(1)}, bf16[512,128]{1,0:T(8,128)(2,1)S(1)}, u32[]{:S(2)}, u32[]{:S(2)}) collective-permute-start(bf16[512,128]{1,0:T(8,128)(2,1)S(1)} %collective-permute-done.args_1_), channel_id=1, source_target_pairs={{0,8},{8,0},{16,24},{24,16},{32,40},{40,32},{48,56},{56,48},{64,72... | collective-permute-start | bytes 393224 | tf_op jit(solution)/shard_map/ppermute | solution.py:380
  64.6 6.0 %collective-permute-start.7 = (bf16[256,128]{1,0:T(8,128)(2,1)S(1)}, bf16[256,128]{1,0:T(8,128)(2,1)S(1)}, u32[]{:S(2)}, u32[]{:S(2)}) collective-permute-start(bf16[256,128]{1,0:T(8,128)(2,1)S(1)} %get-tuple-element.9.args_8_), channel_id=1, source_target_pairs={{0,32},{8,40},{16,48},{24,56},{32,0},{40,8},{48,16},{56,24},{64,96... | collective-permute-start | bytes 196616 | tf_op jit(solution)/shard_map/ppermute | solution.py:377
  70.6 10.5 %collective-permute-start.11 = (bf16[256,128]{1,0:T(8,128)(2,1)S(1)}, bf16[256,128]{1,0:T(8,128)(2,1)S(1)}, u32[]{:S(2)}, u32[]{:S(2)}) collective-permute-start(bf16[256,128]{1,0:T(8,128)(2,1)S(1)} %get-tuple-element.9.args_8_), channel_id=1, source_target_pairs={{0,48},{8,56},{16,0},{24,8},{32,16},{40,24},{48,32},{56,40},{64,11... | collective-permute-start | bytes 196616 | tf_op jit(solution)/shard_map/ppermute | solution.py:377
  71.1 6.7 %collective-permute-start.9 = (bf16[256,128]{1,0:T(8,128)(2,1)S(1)}, bf16[256,128]{1,0:T(8,128)(2,1)S(1)}, u32[]{:S(2)}, u32[]{:S(2)}) collective-permute-start(bf16[256,128]{1,0:T(8,128)(2,1)S(1)} %get-tuple-element.9.args_8_), channel_id=1, source_target_pairs={{0,16},{8,24},{16,32},{24,40},{32,48},{40,56},{48,0},{56,8},{64,80... | collective-permute-start | bytes 196616 | tf_op jit(solution)/shard_map/ppermute | solution.py:377
  74.2 10.7 %collective-permute-start.8 = (bf16[80,512]{1,0:T(8,128)(2,1)S(1)}, bf16[80,512]{1,0:T(8,128)(2,1)S(1)}, u32[]{:S(2)}, u32[]{:S(2)}) collective-permute-start(bf16[80,512]{1,0:T(8,128)(2,1)S(1)} %attend.4), channel_id=1, source_target_pairs={{0,32},{8,40},{16,48},{24,56},{32,0},{40,8},{48,16},{56,24},{64,96... | collective-permute-start | bytes 245768 | tf_op jit(solution)/shard_map/ppermute | solution.py:384
  79.4 5.5 %collective-permute-start.10 = (bf16[80,512]{1,0:T(8,128)(2,1)S(1)}, bf16[80,512]{1,0:T(8,128)(2,1)S(1)}, u32[]{:S(2)}, u32[]{:S(2)}) collective-permute-start(bf16[80,512]{1,0:T(8,128)(2,1)S(1)} %attend.5), channel_id=1, source_target_pairs={{0,48},{8,56},{16,0},{24,8},{32,16},{40,24},{48,32},{56,40},{64,11... | collective-permute-start | bytes 245768 | tf_op jit(solution)/shard_map/ppermute | solution.py:384
  81.0 21.7 %collective-permute-start.13 = (bf16[8,64,1024]{2,1,0:T(8,128)(2,1)S(1)}, bf16[8,64,1024]{2,1,0:T(8,128)(2,1)S(1)}, u32[]{:S(2)}, u32[]{:S(2)}) collective-permute-start(bf16[8,64,1024]{2,1,0:T(8,128)(2,1)S(1)} %all-to-all-done.2._.w_mine), channel_id=1, source_target_pairs={{0,8},{8,0},{16,24},{24,16},{32,40},{40,32},{48,56},{56,48},{64,72... | collective-permute-start | bytes 3145736 | tf_op jit(solution)/shard_map/ppermute | solution.py:388
  82.7 20.1 %copy-start.9 = (f32[1024]{0:T(1024)S(1)}, f32[1024]{0:T(1024)}, u32[]{:S(2)}) copy-start(f32[1024]{0:T(1024)} %param.16) | copy-start | bytes 12292
  82.7 4.9 %collective-permute-start.12 = (bf16[80,512]{1,0:T(8,128)(2,1)S(1)}, bf16[80,512]{1,0:T(8,128)(2,1)S(1)}, u32[]{:S(2)}, u32[]{:S(2)}) collective-permute-start(bf16[80,512]{1,0:T(8,128)(2,1)S(1)} %attend.6), channel_id=1, source_target_pairs={{0,16},{8,24},{16,32},{24,40},{32,48},{40,56},{48,0},{56,8},{64,80... | collective-permute-start | bytes 245768 | tf_op jit(solution)/shard_map/ppermute | solution.py:384
  84.9 18.8 %copy-start.6 = (bf16[1024,1024]{1,0:T(8,128)(2,1)S(1)}, bf16[1024,1024]{1,0:T(8,128)(2,1)}, u32[]{:S(2)}) copy-start(bf16[1024,1024]{1,0:T(8,128)(2,1)} %weight.1) | copy-start | bytes 6291460
  84.9 18.8 %copy-start.7 = (f32[8,1024]{1,0:T(8,128)S(1)}, f32[8,1024]{1,0:T(8,128)}, u32[]{:S(2)}) copy-start(f32[8,1024]{1,0:T(8,128)} %scale.1) | copy-start | bytes 98308
  84.9 18.8 %copy-start.8 = (f32[8,1024]{1,0:T(8,128)S(1)}, f32[8,1024]{1,0:T(8,128)}, u32[]{:S(2)}) copy-start(f32[8,1024]{1,0:T(8,128)} %shift.1) | copy-start | bytes 98308
